TPU v7x, 32 devices: a whole 2x2x4 slice. The times are simulated.
32 devices in a mesh: seq: 8 (over z, y), rep: 4 (over x, core).
Axes of the slice: x: 2, y: 2, z: 4, core: 2. Of those that a mesh axis runs over, the one named last changes fastest.
Arguments:
- inputs: bfloat16 [4, 1024, 1024], P('rep', 'seq'), may hold values from -6 to 6
- weight_t: bfloat16 [3072, 1024], P('seq', 'rep'), may hold values from -0.1875 to 0.1875
- states: float32 [4, 1024, 1024], P('rep', 'seq'), may hold values from -0.9 to 0.9
- doc_ids: int32 [4, 1024], P('rep', 'seq'), may hold values from 0 to 3, never falling along the last dimension, each value on 1 to 512 neighbouring positions
- recur: float32 [3, 1024], replicated, may hold values from -1 to 1
- bias: float32 [3, 1024], replicated, may hold values from -8 to 3, as said below
- out_grad: bfloat16 [4, 1024, 1024], P('rep', 'seq'), may hold values from -6 to 6
Outputs:
- input_grad: bfloat16 [4, 1024, 1024], P('rep', 'seq')
- weight_grad: float32 [3072, 1024], P('seq', 'rep')
- param_grad: float32 [6, 1024], replicated
Inputs may be any that keep to these rules, and one draw needn't show every extreme that they name: `doc_ids`: within each sequence the numbers never fall; every document has 1 to 512 tokens, and some document has exactly 512. `bias`: row 0 lies between -8 and -1, rows 1 and 2 between -3 and 3.
All inputs are finite; a program needn't handle non-finite values.
Results may differ from a plain program's by a relative error of at most 0.0095.
Values may be sent and summed in bfloat16 or wider, within the bound.
A program may use at most 128 MiB of HBM per device.

v0:
```python
import functools
import math

import jax
import jax.numpy as jnp
from jax import lax
from jax.experimental import pallas as pl
from jax.experimental.pallas import tpu as pltpu
from jax.sharding import PartitionSpec as P

F32 = jnp.float32
BF16 = jnp.bfloat16
GATES = 3


def shifted(block, axis, distance):
    devices = range(lax.axis_size(axis))
    route = [(i - distance, i) for i in devices if i - distance in devices]
    return lax.ppermute(block, axis, route)


def compose(earlier, later):
    return (later[0] * earlier[0], later[1] + later[0] * earlier[1])


def by_tokens(inputs, weight_t, states, doc_ids, recur, bias, out_grad):
    feats = inputs[0]
    hidden_now = states[0]
    ids_float = doc_ids[0].astype(F32)
    count = feats.shape[0]
    width = hidden_now.shape[1]
    columns = lax.all_gather(weight_t, "rep", axis=1, tiled=True)
    contract_last = (((1,), (1,)), ((), ()))
    full_weight = lax.all_gather(columns, "seq", axis=0, tiled=True)
    preact = lax.dot_general(feats, full_weight, contract_last, preferred_element_type=F32)
    tail_state, tail_id = shifted((hidden_now[-1:], ids_float[-1:]), "seq", 1)
    first_same = jnp.where(
        (ids_float[0] == tail_id[0]) & (lax.axis_index("seq") > 0), 1.0, 0.0
    ).astype(F32)
    same = jnp.concatenate([first_same[None], (ids_float[1:] == ids_float[:-1]).astype(F32)])
    prior = jnp.concatenate([tail_state, hidden_now[:-1]], 0) * same[:, None]
    gate_z = jax.nn.sigmoid(preact[:, :width] + recur[0] * prior + bias[0])
    gate_r = jax.nn.sigmoid(preact[:, width : 2 * width] + recur[1] * prior + bias[1])
    gate_c = jnp.tanh(preact[:, 2 * width :] + recur[2] * gate_r * prior + bias[2])
    jacobian = same[:, None] * (
        1.0
        - gate_z
        + (gate_c - prior) * gate_z * (1.0 - gate_z) * recur[0]
        + gate_z
        * (1.0 - gate_c * gate_c)
        * recur[2]
        * (gate_r + prior * gate_r * (1.0 - gate_r) * recur[1])
    )
    upstream = out_grad[0].astype(F32)
    jac_rows, up_rows = (
        lax.all_to_all(jacobian.T, "seq", split_axis=0, concat_axis=1, tiled=True),
        lax.all_to_all(upstream.T, "seq", split_axis=0, concat_axis=1, tiled=True),
    )
    factor = jnp.concatenate([jac_rows[:, 1:], jnp.zeros((jac_rows.shape[0], 1), F32)], 1)
    _, adjoint_rows = lax.associative_scan(compose, (factor, up_rows), reverse=True, axis=1)
    adjoint = lax.all_to_all(adjoint_rows, "seq", split_axis=1, concat_axis=0, tiled=True).T
    grad_z = adjoint * (gate_c - prior) * gate_z * (1.0 - gate_z)
    grad_c = adjoint * gate_z * (1.0 - gate_c * gate_c)
    grad_r = grad_c * recur[2] * prior * gate_r * (1.0 - gate_r)
    grad_pre = jnp.concatenate([grad_z, grad_r, grad_c], 1).astype(BF16)
    input_grad = jnp.dot(grad_pre, full_weight, preferred_element_type=F32)
    tokens_all = count * inputs.shape[0] * lax.axis_size("seq") * lax.axis_size("rep")
    normal_factor = 1.0 / math.sqrt(tokens_all)
    row_share = lax.psum_scatter(
        lax.dot_general(grad_pre, feats, (((0,), (0,)), ((), ())), preferred_element_type=F32),
        "seq",
        scatter_dimension=0,
        tiled=True,
    )
    weight_grad = (
        lax.psum_scatter(row_share.astype(BF16), "rep", scatter_dimension=1, tiled=True).astype(F32)
        * normal_factor
    )
    stats = jnp.stack(
        [
            grad_z.sum(0),
            grad_r.sum(0),
            grad_c.sum(0),
            (grad_z * prior).sum(0),
            (grad_r * prior).sum(0),
            (grad_c * gate_r * prior).sum(0),
        ]
    )
    param_grad = lax.psum(stats, ("seq", "rep")) * normal_factor
    return (input_grad.astype(BF16)[None], weight_grad, param_grad)


def kernel(
    ns, nr, feats, weight, states, ids, recur, bias, upstream,
    out_in, out_w, out_p,
    pay_src, pay, ids_src, ids_all, tail_src, tail_in, x_all, w_all, prev, ids_col, up, jac,
    co_z, co_r, co_c, rprior, prior_all,
    scan_a, scan_b, carry, seg_out, seg_in, lam, grads, part_out, part_in, part_keep, fin_out, fin_in,
    wg_out, wg_in, st_out, st_in,
    x_s0, x_sx, x_sy, x_sd, x_r, w_s, w_r, p_s, p_r, i_s, i_r, e_s, e_r, c_s, c_r, d_s, d_r, f_s, f_r,
    g_s, g_r, t_s, t_r,
):
    T, DI = feats.shape
    H = states.shape[1]
    nh, nz, nx = 2 * nr, ns // 2, nr // 2
    hb, cw = H // nh, DI // nr
    s, r = lax.axis_index("seq"), lax.axis_index("rep")
    z, y, x, c = s // 2, s % 2, r // 2, r % 2
    k = 2 * r + y
    me = s * nr + r
    unsent = []

    def place(a, b):
        return {"seq": a, "rep": b}

    def at(plane, j):
        return place(2 * plane + j % 2, j // 2)

    def send(src, dst, ssem, rsem, where):
        pltpu.make_async_remote_copy(
            src_ref=src, dst_ref=dst, send_sem=ssem, recv_sem=rsem,
            device_id=where, device_id_type=pl.DeviceIdType.MESH,
        ).start()

    def local(src, dst, rsem):
        pltpu.make_async_copy(src, dst, rsem).start()

    def landed(dst, sem):
        pltpu.make_async_copy(dst, dst, sem).wait()

    def send_if(allowed, src, dst, ssem, rsem, where):
        @pl.when(allowed)
        def _():
            send(src, dst, ssem, rsem, where)

        unsent.append((allowed, src, ssem))

    def send_or_local(src, dst, ssem, rsem, where, here):
        send_if(jnp.logical_not(here), src, dst, ssem, rsem, where)

        @pl.when(here)
        def _():
            local(src, dst, rsem)

    def rows(ref, block, count):
        return ref.at[pl.ds(pl.multiple_of(block * count, count), count), :]

    barrier = pltpu.get_barrier_semaphore()

    def greet(d, _):
        @pl.when(d != me)
        def _():
            pl.semaphore_signal(
                barrier, inc=1, device_id=place(d // nr, d % nr), device_id_type=pl.DeviceIdType.MESH
            )

        return 0

    lax.fori_loop(0, ns * nr, greet, 0)
    for j in range(nh):
        pay_src[j, :, :hb] = states[:, j * hb : (j + 1) * hb].astype(BF16)
        pay_src[j, :, hb:] = upstream[:, j * hb : (j + 1) * hb]
        tail_src[j, 0:8, :] = states[T - 8 : T, j * hb : (j + 1) * hb]
        tail_src[j, 8:16, :] = jnp.broadcast_to(ids[0:1, T - 1 : T].astype(F32), (8, hb))
    ids_src[...] = jnp.broadcast_to(ids[...].astype(F32), ids_src.shape)

    pl.semaphore_wait(barrier, ns * nr - 1)

    steps = sorted(range(nz), key=lambda step: -min(step, nz - step))
    for step in steps:
        plane = (z + step) % nz
        for i in range(GATES):
            b = GATES * s + i
            g, j = b // nh, b % nh
            dst = w_all.at[
                pl.ds(pl.multiple_of(g * hb, hb), hb), pl.ds(pl.multiple_of(r * cw, cw), cw)
            ]
            here = jnp.logical_and(step == 0, j == k)
            send_or_local(
                weight.at[i * hb : (i + 1) * hb, :], dst, w_s.at[i * nz + step],
                w_r.at[g * nr + r], at(plane, j), here,
            )
    partner = place(s, r + 1 - 2 * c)
    local(feats, rows(x_all, k, T), x_s0)

    def share(step, src, dx, dy):
        x0, y0 = (x + dx) % nx, (y + dy) % 2
        slot = 2 * (2 * x0 + c) + y0
        dst = rows(x_all, slot, T)
        src = dst if src is None else src
        if dy == 0 or dx == 0:
            for other in range(1, nx):
                if dx == 0:
                    allowed = True if dy == 0 else c == 0
                    send_if(
                        allowed, src, dst, x_sx.at[step * nx + other], x_r.at[slot],
                        place(s, 2 * ((x + other) % nx) + c),
                    )
            if dy == 0:
                allowed = True if dx == 0 else c == 1
                send_if(allowed, src, dst, x_sy.at[step], x_r.at[slot], place(2 * z + 1 - y, r))
        send_if(True, src, dst, x_sd.at[step], x_r.at[slot], partner)

    share(0, feats, 0, 0)

    for j in range(nh):
        send_or_local(ids_src, ids_all.at[k], i_s.at[j], i_r.at[k], at(z, j), k == j)
        send_or_local(pay_src.at[j], pay.at[k], p_s.at[j], p_r.at[k], at(z, j), k == j)
        send_if(
            jnp.logical_and(y == 1, z < nz - 1), tail_src.at[j], tail_in.at[r], e_s.at[j], e_r.at[r],
            at(z + 1, j),
        )

    hops = [(dx, dy) for dx in range(nx) for dy in range(2)]
    hops.sort(key=lambda hop: (hop[0] > 0) + hop[1])
    for step, (dx, dy) in enumerate(hops):
        if step > 0:
            slot = 2 * (2 * ((x + dx) % nx) + c) + (y + dy) % 2
            landed(rows(x_all, slot, T), x_r.at[slot])
            share(step, None, dx, dy)

    stride = T + 8
    for m in range(nh):
        base = m * stride + 8
        landed(ids_all.at[m], i_r.at[m])
        landed(pay.at[m], p_r.at[m])
        prev[base : base + T, :] = pay[m, :, :hb].astype(F32)
        up[m * T : (m + 1) * T, :] = pay[m, :, hb:].astype(F32)
        ids_col[base : base + T, :] = jnp.broadcast_to(ids_all[m, 0:1, :], (hb, T)).T
        if m % 2:
            before = base - stride + T
            prev[base - 8 : base, :] = prev[before - 8 : before, :]
            ids_col[base - 8 : base, :] = ids_col[before - 8 : before, :]
        else:

            @pl.when(z > 0)
            def _():
                landed(tail_in.at[m // 2], e_r.at[m // 2])
                prev[base - 8 : base, :] = tail_in[m // 2, 0:8, :]
                ids_col[base - 8 : base, :] = tail_in[m // 2, 8:16, :]

            @pl.when(z == 0)
            def _():
                prev[base - 8 : base, :] = jnp.zeros((8, hb), F32)
                ids_col[base - 8 : base, :] = jnp.full((8, hb), -1.0, F32)

    for g in range(GATES):
        for col in range(nr):
            landed(
                w_all.at[g * hb : (g + 1) * hb, col * cw : (col + 1) * cw], w_r.at[g * nr + col]
            )
    landed(rows(x_all, k, T), x_s0)
    for x0 in range(nx):
        for y0 in range(2):
            slot = 2 * (2 * x0 + 1 - c) + y0
            landed(rows(x_all, slot, T), x_r.at[slot])

    group = pl.ds(pl.multiple_of(k * hb, hb), hb)
    rz, rr, rc = (recur[i : i + 1, group] for i in range(GATES))
    bz, br, bc = (bias[i : i + 1, group] for i in range(GATES))
    for m in range(nh):
        span = slice(m * T, (m + 1) * T)
        base = m * stride + 8
        pre = lax.dot_general(
            x_all[span, :], w_all[...], (((1,), (1,)), ((), ())), preferred_element_type=F32
        )
        same = jnp.where(
            ids_col[base : base + T, :] == ids_col[base - 1 : base - 1 + T, :], 1.0, 0.0
        )
        prior = prev[base - 1 : base - 1 + T, :] * same
        gz = jax.nn.sigmoid(pre[:, :hb] + rz * prior + bz)
        gr = jax.nn.sigmoid(pre[:, hb : 2 * hb] + rr * prior + br)
        rp = gr * prior
        gc = jnp.tanh(pre[:, 2 * hb :] + rc * rp + bc)
        az = (gc - prior) * gz * (1.0 - gz)
        ac = gz * (1.0 - gc * gc)
        slope = rp * (1.0 - gr)
        acr = ac * rc
        co_z[span, :] = az
        co_c[span, :] = ac
        co_r[span, :] = acr * slope
        rprior[span, :] = rp
        prior_all[span, :] = prior
        jac[span, :] = same * (1.0 - gz + az * rz + acr * (gr + slope * rr))

    def back(i, state):
        a, b = state
        t = T - 1 - i
        f = jac[pl.ds(t, nh, stride=T), :]
        b = b + up[pl.ds(t, nh, stride=T), :]
        scan_a[t] = a
        scan_b[t] = b
        return f * a, f * b

    a, b = lax.fori_loop(0, T, back, (jnp.ones((nh, hb), F32), jnp.zeros((nh, hb), F32)), unroll=8)
    seg_out[...] = jnp.zeros(seg_out.shape, F32)
    for o in range(nr):
        first, second = slice(2 * o, 2 * o + 1), slice(2 * o + 1, 2 * o + 2)
        seg_out[0, o : o + 1, :] = a[first, :] * a[second, :]
        seg_out[1, o : o + 1, :] = b[first, :] + a[first, :] * b[second, :]
    for plane in range(nz - 1):
        send_if(plane < z, seg_out, seg_in.at[z], c_s.at[plane], c_r.at[z], at(plane, k))
    carry[...] = jnp.zeros(carry.shape, F32)
    for plane in reversed(range(1, nz)):

        @pl.when(plane > z)
        def _():
            landed(seg_in.at[plane], c_r.at[plane])
            carry[0:nr, :] = seg_in[plane, 1, 0:nr, :] + seg_in[plane, 0, 0:nr, :] * carry[0:nr, :]

    into = carry[0:nr, :]
    carry_rows = []
    for o in range(nr):
        later = into[o : o + 1, :]
        second = slice(2 * o + 1, 2 * o + 2)
        carry_rows += [b[second, :] + a[second, :] * later, later]
    carried = jnp.concatenate(carry_rows, 0)

    def finish(t, _):
        lam[pl.ds(t, nh, stride=T), :] = scan_b[t] + scan_a[t] * carried
        return 0

    lax.fori_loop(0, T, finish, 0, unroll=8)

    sums = [jnp.zeros((1, hb), F32) for _ in range(6)]
    for m in range(nh):
        span = slice(m * T, (m + 1) * T)
        prior = prior_all[span, :]
        adj = lam[span, :]
        grad_z = adj * co_z[span, :]
        grad_r = adj * co_r[span, :]
        grad_c = adj * co_c[span, :]
        grads[span, :hb] = grad_z.astype(BF16)
        grads[span, hb : 2 * hb] = grad_r.astype(BF16)
        grads[span, 2 * hb :] = grad_c.astype(BF16)
        terms = (grad_z, grad_r, grad_c, grad_z * prior, grad_r * prior, grad_c * rprior[span, :])
        sums = [total + jnp.sum(term, 0, keepdims=True) for total, term in zip(sums, terms)]
    for i in range(6):
        st_out[i : i + 1, :] = sums[i]
    st_out[6:8, :] = jnp.zeros((2, hb), F32)

    slot = k * nz + z
    st_in[slot] = st_out[...]

    def tell(d, _):
        @pl.when(d != me)
        def _():
            send(st_out, st_in.at[slot], t_s.at[d], t_r.at[slot], place(d // nr, d % nr))

        return 0

    lax.fori_loop(0, ns * nr, tell, 0)

    for g in range(GATES):
        wg_out[g] = lax.dot_general(
            grads[:, g * hb : (g + 1) * hb], x_all[...], (((0,), (0,)), ((), ())),
            preferred_element_type=F32,
        ).astype(BF16)
        b = g * nh + k
        owner, i = b // GATES, b % GATES
        for col in range(nr):
            here = jnp.logical_and(owner == s, r == col)
            send_or_local(
                wg_out.at[g, :, col * cw : (col + 1) * cw], wg_in.at[z * GATES + i],
                g_s.at[g * nr + col], g_r.at[z * GATES + i], place(owner, col), here,
            )

    chips = [(x0, y0) for x0 in range(nx) for y0 in range(2)]
    for n, (x0, y0) in enumerate(chips):
        part_out[n] = jnp.dot(
            rows(grads, 2 * (2 * x0 + 1 - c) + y0, T)[...], w_all[...], preferred_element_type=F32
        ).astype(BF16)
        send_if(True, part_out.at[n], part_in.at[n], d_s.at[n], d_r.at[n], partner)
    for n, (x0, y0) in enumerate(chips):
        part_keep[n] = jnp.dot(
            rows(grads, 2 * (2 * x0 + c) + y0, T)[...], w_all[...], preferred_element_type=F32
        )
    chip = 2 * x + y
    for n, (x0, y0) in enumerate(chips):
        landed(part_in.at[n], d_r.at[n])
        fin_out[n] = (part_keep[n] + part_in[n].astype(F32)).astype(BF16)
        send_or_local(
            fin_out.at[n], fin_in.at[chip], f_s.at[n], f_r.at[chip],
            place(2 * z + y0, 2 * x0 + c), chip == n,
        )

    scale = 1.0 / math.sqrt(ns * nr * T)

    def heard(d, _):
        @pl.when(d != slot)
        def _():
            landed(st_in.at[d], t_r.at[d])

        return 0

    lax.fori_loop(0, ns * nr, heard, 0)
    for j in range(nh):
        total = st_in[j * nz]
        for other in range(1, nz):
            total = total + st_in[j * nz + other]
        out_p[:, j * hb : (j + 1) * hb] = total[:6] * scale

    total = None
    for n in range(len(chips)):
        landed(fin_in.at[n], f_r.at[n])
        term = fin_in[n].astype(F32)
        total = term if total is None else total + term
    out_in[...] = total.astype(BF16)

    for i in range(GATES):
        total = None
        for other in range(nz):
            landed(wg_in.at[other * GATES + i], g_r.at[other * GATES + i])
            term = wg_in[other * GATES + i].astype(F32)
            total = term if total is None else total + term
        out_w[i * hb : (i + 1) * hb, :] = total * scale

    def told(d, _):
        @pl.when(d != me)
        def _():
            landed(st_out, t_s.at[d])

        return 0

    lax.fori_loop(0, ns * nr, told, 0)
    for sent, src, sem in unsent:
        if sent is True:
            landed(src, sem)
        else:

            @pl.when(sent)
            def _():
                landed(src, sem)


def by_hidden(ns, nr, inputs, weight_t, states, doc_ids, recur, bias, out_grad):
    T, DI = inputs.shape[1:]
    H = states.shape[2]
    nh, nz, nx = 2 * nr, ns // 2, nr // 2
    hb, cw = H // nh, DI // nr
    L = nh * T
    vm = pltpu.VMEM
    scratch = [
        vm((nh, T, 2 * hb), BF16),
        vm((nh, T, 2 * hb), BF16),
        vm((8, T), F32),
        vm((nh, 8, T), F32),
        vm((nh, 16, hb), F32),
        vm((nr, 16, hb), F32),
        vm((L, DI), BF16),
        vm((GATES * hb, DI), BF16),
        vm((L + 8 * nh, hb), F32),
        vm((L + 8 * nh, hb), F32),
        vm((L, hb), F32),
        vm((L, hb), F32),
        vm((L, hb), F32),
        vm((L, hb), F32),
        vm((L, hb), F32),
        vm((L, hb), F32),
        vm((L, hb), F32),
        vm((T, nh, hb), F32),
        vm((T, nh, hb), F32),
        vm((nh, hb), F32),
        vm((2, 8, hb), F32),
        vm((nz, 2, 8, hb), F32),
        vm((L, hb), F32),
        vm((L, GATES * hb), BF16),
        vm((nr, T, DI), BF16),
        vm((nr, T, DI), BF16),
        vm((nr, T, DI), F32),
        vm((nr, T, DI), BF16),
        vm((nr, T, DI), BF16),
        vm((GATES, hb, DI), BF16),
        vm((nz * GATES, hb, cw), BF16),
        vm((8, hb), F32),
        vm((ns * nr, 8, hb), F32),
    ]
    dma = pltpu.SemaphoreType.DMA
    counts = [
        None, nr * nx, nr, nr, nh, GATES * nz, GATES * nr, nh, nh, nh, nh, nh, nr, nz, nz, nr, nr, nr, nr,
        GATES * nr, GATES * nz, ns * nr, ns * nr,
    ]
    sems = [dma if n is None else dma((n,)) for n in counts]
    whole = pl.BlockSpec(memory_space=pltpu.VMEM)
    out_in, out_w, out_p = pl.pallas_call(
        functools.partial(kernel, ns, nr),
        out_shape=(
            jax.ShapeDtypeStruct((T, DI), BF16),
            jax.ShapeDtypeStruct(weight_t.shape, F32),
            jax.ShapeDtypeStruct((6, H), F32),
        ),
        in_specs=[whole] * 7,
        out_specs=(whole,) * 3,
        scratch_shapes=scratch + sems,
        compiler_params=pltpu.CompilerParams(
            collective_id=0, has_side_effects=True, vmem_limit_bytes=56 * 1024 * 1024
        ),
    )(inputs[0], weight_t, states[0], doc_ids, recur, bias, out_grad[0])
    return out_in[None], out_w, out_p


def fits(ns, nr, inputs, weight_t, states):
    parts, L, DI = inputs.shape
    H = states.shape[2]
    return (
        parts == nr
        and ns == 2 * nr
        and ns % 8 == 0
        and ns == 8
        and H % (ns * 128) == 0
        and DI % (nr * 128) == 0
        and L % (ns * 128) == 0
        and L * DI <= 1 << 21
    )


def solution(mesh):
    ns, nr = mesh.shape["seq"], mesh.shape["rep"]
    placed = (
        P("rep", "seq", None),
        P("seq", "rep"),
        P("rep", "seq", None),
        P("rep", "seq"),
        P(),
        P(),
        P("rep", "seq", None),
    )

    def run(inputs, weight_t, states, doc_ids, recur, bias, out_grad):
        kernelized = fits(ns, nr, inputs, weight_t, states)
        body = functools.partial(by_hidden, ns, nr) if kernelized else by_tokens
        return jax.shard_map(
            body,
            mesh=mesh,
            in_specs=placed,
            out_specs=(P("rep", "seq", None), P("seq", "rep"), P()),
            check_vma=False,
        )(inputs, weight_t, states, doc_ids, recur, bias, out_grad)

    return run
```

profile of v0, /device:TPU:27, one launch (start us, length us, event | category | flops | bytes accessed | tf_op | source)
XLA Modules:
  0.0 72.2 jit_solution(2365252933304439288)
XLA Ops:
  0.6 68.4 %shard_map.94 = (bf16[128,1024]{1,0:T(8,128)(2,1)}, f32[384,256]{1,0:T(8,128)}, f32[6,1024]{1,0:T(8,128)}) custom-call(bf16[128,1024]{1,0:T(8,128)(2,1)} %bitcast.6, bf16[384,256]{1,0:T(8,128)(2,1)} %weight.1, f32[128,1024]{1,0:T(8,128)} %bitcast.4, s32[1,128]{1,0:T(1,128)} %ids.1, f32[3,1024]{1,0:T(4,128)} %recur.1, f32[3,1024]{1,0:T(4,128)} %bias.1, ...), custom_call_target="tpu_custom_call" | custom-call | tf_op jit(solution)/shard_map/pallas_call | solution.py:485
  69.1 0.0 copy-start
  69.1 1.7 %copy.13 = bf16[1,128,1024]{2,1,0:T(8,128)(2,1)} copy(bf16[1,128,1024]{2,1,0:T(8,128)(2,1)} %bitcast.5) | data formatting | bytes 524288
  70.8 0.0 copy-done
  70.8 0.0 copy-start.1
  70.8 0.7 %copy.14 = f32[384,256]{1,0:T(8,128)} copy(f32[384,256]{1,0:T(8,128)S(1)} %copy-done) | data formatting | bytes 786432
  71.5 0.0 copy-done.1
  71.5 0.6 copy.15
Async XLA Ops:
  69.1 1.7 %copy-start = (f32[384,256]{1,0:T(8,128)S(1)}, f32[384,256]{1,0:T(8,128)}, u32[]{:S(2)}) copy-start(f32[384,256]{1,0:T(8,128)} %get-tuple-element.13) | copy-start | bytes 1179652
  70.8 0.8 %copy-start.1 = (f32[6,1024]{1,0:T(8,128)S(1)}, f32[6,1024]{1,0:T(8,128)}, u32[]{:S(2)}) copy-start(f32[6,1024]{1,0:T(8,128)} %get-tuple-element.14) | copy-start | bytes 73732
where the time goes:
time: 72.4 us; the launch traced here: 72.2 us
  Pallas kernels  68.4 us (94%)
  local copies, waits for them, and re-layouts  3.1 us (4%)
    pallas_call x1, Pallas kernels, by_hidden(): pl.pallas_call(functools.partial(kernel, ns, nr), out_shape=(jax.ShapeDty...  68.4 us
    unnamed x7, local copies, waits for them, and re-layouts  3.1 us

commit v1 on v0

--- a/solution.py
+++ b/solution.py
@@ -433,6 +433,15 @@
                 landed(src, sem)
 
 
+def flush(in_a, in_b, in_c, out_a, out_b, out_c, sems):
+    pairs = [(in_a, out_a), (in_b, out_b), (in_c, out_c)]
+    copies = [pltpu.make_async_copy(a, b, sems.at[i]) for i, (a, b) in enumerate(pairs)]
+    for copy in copies:
+        copy.start()
+    for copy in copies:
+        copy.wait()
+
+
 def by_hidden(ns, nr, inputs, weight_t, states, doc_ids, recur, bias, out_grad):
     T, DI = inputs.shape[1:]
     H = states.shape[2]
@@ -485,9 +494,9 @@
     out_in, out_w, out_p = pl.pallas_call(
         functools.partial(kernel, ns, nr),
         out_shape=(
-            jax.ShapeDtypeStruct((T, DI), BF16),
-            jax.ShapeDtypeStruct(weight_t.shape, F32),
-            jax.ShapeDtypeStruct((6, H), F32),
+            pltpu.VMEM((T, DI), BF16),
+            pltpu.VMEM(weight_t.shape, F32),
+            pltpu.VMEM((6, H), F32),
         ),
         in_specs=[whole] * 7,
         out_specs=(whole,) * 3,
@@ -496,6 +505,14 @@
             collective_id=0, has_side_effects=True, vmem_limit_bytes=56 * 1024 * 1024
         ),
     )(inputs[0], weight_t, states[0], doc_ids, recur, bias, out_grad[0])
+    shapes = ((T, DI), BF16), (weight_t.shape, F32), ((6, H), F32)
+    out_in, out_w, out_p = pl.pallas_call(
+        flush,
+        out_shape=tuple(jax.ShapeDtypeStruct(*one) for one in shapes),
+        in_specs=[whole] * 3,
+        out_specs=(pl.BlockSpec(memory_space=pltpu.HBM),) * 3,
+        scratch_shapes=[dma((3,))],
+    )(*(pltpu.with_memory_space_constraint(one, pltpu.VMEM) for one in (out_in, out_w, out_p)))
     return out_in[None], out_w, out_p
 
 

time: 72.4 us -> 69.2 us (0.956)
  local copies, waits for them, and re-layouts: 3.1 us -> 0 us
    unnamed x7 -> x0, local copies, waits for them, and re-layouts: 3.1 us -> none
    pallas_call x1 -> x2, Pallas kernels: 68.4 us -> 68.4 us  [the longest x1 67.6 us: by_hidden(): pl.pallas_call(functools.partial(kernel, ns, nr), out_shape=(pltpu.VMEM((...]
where the time goes in v1:
time: 69.2 us; the launch traced here: 69.1 us
  Pallas kernels  68.4 us (99%)
    pallas_call x1, Pallas kernels, by_hidden(): pl.pallas_call(functools.partial(kernel, ns, nr), out_shape=(pltpu.VMEM((...  67.6 us

profile of v1, /device:TPU:27, one launch (start us, length us, event | category | flops | bytes accessed | tf_op | source)
XLA Modules:
  0.0 69.1 jit_solution(1981092368927046314)
XLA Ops:
  0.6 67.6 %shard_map.94 = (bf16[128,1024]{1,0:T(8,128)(2,1)S(1)}, f32[384,256]{1,0:T(8,128)S(1)}, f32[6,1024]{1,0:T(8,128)S(1)}) custom-call(bf16[128,1024]{1,0:T(8,128)(2,1)} %bitcast.5, bf16[384,256]{1,0:T(8,128)(2,1)} %weight.1, f32[128,1024]{1,0:T(8,128)} %bitcast.4, s32[1,128]{1,0:T(1,128)} %ids.1, f32[3,1024]{1,0:T(4,128)} %recur.1, f32[3,1024]{1,0:T(4,128)} %bias.1, ...), custom_call_target="tpu_custom_call" | custom-call | tf_op jit(solution)/shard_map/pallas_call | solution.py:494
  68.2 0.9 %shard_map.95 = (bf16[128,1024]{1,0:T(8,128)(2,1)}, f32[384,256]{1,0:T(8,128)}, f32[6,1024]{1,0:T(8,128)}) custom-call(bf16[128,1024]{1,0:T(8,128)(2,1)S(1)} %get-tuple-element.9.in_a, f32[384,256]{1,0:T(8,128)S(1)} %get-tuple-element.10.in_b, f32[6,1024]{1,0:T(8,128)S(1)} %get-tuple-element.11.in_c), custom_call_target="tpu_custom_call" | custom-call | tf_op jit(solution)/shard_map/pallas_call | solution.py:509

commit v2 on v1

--- a/solution.py
+++ b/solution.py
@@ -96,9 +96,9 @@
     pay_src, pay, ids_src, ids_all, tail_src, tail_in, x_all, w_all, prev, ids_col, up, jac,
     co_z, co_r, co_c, rprior, prior_all,
     scan_a, scan_b, carry, seg_out, seg_in, lam, grads, part_out, part_in, part_keep, fin_out, fin_in,
-    wg_out, wg_in, st_out, st_in,
-    x_s0, x_sx, x_sy, x_sd, x_r, w_s, w_r, p_s, p_r, i_s, i_r, e_s, e_r, c_s, c_r, d_s, d_r, f_s, f_r,
-    g_s, g_r, t_s, t_r,
+    wg_own, wg_out, wg_end, wg_mid, wg_fin, wg_in, st_out, st_z, st_sum, st_all,
+    x_s0, x_sx, x_sy, x_sd, x_r, w_s, w_f, w_r, p_s, p_r, i_s, i_r, e_s, e_r, c_s, c_r, d_s, d_r, f_s, f_r,
+    g_s, g_e, g_m, g_f, g_r, t_s, t_r, u_s, u_r,
 ):
     T, DI = feats.shape
     H = states.shape[1]
@@ -107,7 +107,10 @@
     s, r = lax.axis_index("seq"), lax.axis_index("rep")
     z, y, x, c = s // 2, s % 2, r // 2, r % 2
     k = 2 * r + y
-    me = s * nr + r
+    half, per = nz // 2, GATES * nh // nz
+    high = z // half
+    inner = jnp.logical_or(z == half - 1, z == half)
+    end = high * (nz - 1)
     unsent = []
 
     def place(a, b):
@@ -115,6 +118,9 @@
 
     def at(plane, j):
         return place(2 * plane + j % 2, j // 2)
+
+    def column(plane):
+        return place(2 * plane + y, r)
 
     def send(src, dst, ssem, rsem, where):
         pltpu.make_async_remote_copy(
@@ -147,39 +153,31 @@
 
     barrier = pltpu.get_barrier_semaphore()
 
-    def greet(d, _):
-        @pl.when(d != me)
-        def _():
-            pl.semaphore_signal(
-                barrier, inc=1, device_id=place(d // nr, d % nr), device_id_type=pl.DeviceIdType.MESH
-            )
-
-        return 0
-
-    lax.fori_loop(0, ns * nr, greet, 0)
+    def greet(where):
+        pl.semaphore_signal(barrier, inc=1, device_id=where, device_id_type=pl.DeviceIdType.MESH)
+
+    for j in range(nh):
+        pl.when(j != k)(functools.partial(greet, at(z, j)))
+    for plane in range(nz):
+        pl.when(plane != z)(functools.partial(greet, column(plane)))
     for j in range(nh):
         pay_src[j, :, :hb] = states[:, j * hb : (j + 1) * hb].astype(BF16)
         pay_src[j, :, hb:] = upstream[:, j * hb : (j + 1) * hb]
-        tail_src[j, 0:8, :] = states[T - 8 : T, j * hb : (j + 1) * hb]
-        tail_src[j, 8:16, :] = jnp.broadcast_to(ids[0:1, T - 1 : T].astype(F32), (8, hb))
     ids_src[...] = jnp.broadcast_to(ids[...].astype(F32), ids_src.shape)
 
-    pl.semaphore_wait(barrier, ns * nr - 1)
-
-    steps = sorted(range(nz), key=lambda step: -min(step, nz - step))
-    for step in steps:
-        plane = (z + step) % nz
-        for i in range(GATES):
-            b = GATES * s + i
-            g, j = b // nh, b % nh
-            dst = w_all.at[
-                pl.ds(pl.multiple_of(g * hb, hb), hb), pl.ds(pl.multiple_of(r * cw, cw), cw)
-            ]
-            here = jnp.logical_and(step == 0, j == k)
-            send_or_local(
-                weight.at[i * hb : (i + 1) * hb, :], dst, w_s.at[i * nz + step],
-                w_r.at[g * nr + r], at(plane, j), here,
-            )
+    pl.semaphore_wait(barrier, nh - 1 + nz - 1)
+
+    def piece(g, col):
+        return w_all.at[pl.ds(pl.multiple_of(g * hb, hb), hb), col]
+
+    mine = pl.ds(pl.multiple_of(r * cw, cw), cw)
+    for i in range(GATES):
+        b = GATES * s + i
+        g, j = b // nh, b % nh
+        send_or_local(
+            weight.at[i * hb : (i + 1) * hb, :], piece(g, mine), w_s.at[i], w_r.at[g * nr + r],
+            at(z, j), j == k,
+        )
     partner = place(s, r + 1 - 2 * c)
     local(feats, rows(x_all, k, T), x_s0)
 
@@ -206,18 +204,36 @@
     for j in range(nh):
         send_or_local(ids_src, ids_all.at[k], i_s.at[j], i_r.at[k], at(z, j), k == j)
         send_or_local(pay_src.at[j], pay.at[k], p_s.at[j], p_r.at[k], at(z, j), k == j)
-        send_if(
-            jnp.logical_and(y == 1, z < nz - 1), tail_src.at[j], tail_in.at[r], e_s.at[j], e_r.at[r],
-            at(z + 1, j),
-        )
+
+    def origin(step):
+        plane = (z + (1 - 2 * high) * step + nz) % nz
+        g = (per * plane - k + nh - 1) // nh
+        return plane, g % GATES, jnp.logical_and(g < GATES, nh * g + k < per * (plane + 1))
+
+    def spread(step):
+        plane, g, found = origin(step)
+        for col in range(nr):
+            cols = slice(col * cw, (col + 1) * cw)
+            block, sem = piece(g, cols), w_r.at[g * nr + col]
+            if step == 0:
+                pl.when(found)(functools.partial(landed, block, sem))
+                for n, target in enumerate((half - high, z + 1 - 2 * (z % half))):
+                    send_if(found, block, block, w_f.at[n * nr + col], sem, column(target))
+            else:
+                go = jnp.logical_and(found, inner)
+                pl.when(go)(functools.partial(landed, block, sem))
+                send_if(go, block, block, w_f.at[(step + 1) * nr + col], sem, column(end))
 
     hops = [(dx, dy) for dx in range(nx) for dy in range(2)]
     hops.sort(key=lambda hop: (hop[0] > 0) + hop[1])
+    spread(0)
+    spread(1)
     for step, (dx, dy) in enumerate(hops):
         if step > 0:
             slot = 2 * (2 * ((x + dx) % nx) + c) + (y + dy) % 2
             landed(rows(x_all, slot, T), x_r.at[slot])
             share(step, None, dx, dy)
+    spread(2)
 
     stride = T + 8
     for m in range(nh):
@@ -229,26 +245,36 @@
         ids_col[base : base + T, :] = jnp.broadcast_to(ids_all[m, 0:1, :], (hb, T)).T
         if m % 2:
             before = base - stride + T
+            o = m // 2
             prev[base - 8 : base, :] = prev[before - 8 : before, :]
             ids_col[base - 8 : base, :] = ids_col[before - 8 : before, :]
-        else:
-
-            @pl.when(z > 0)
-            def _():
-                landed(tail_in.at[m // 2], e_r.at[m // 2])
-                prev[base - 8 : base, :] = tail_in[m // 2, 0:8, :]
-                ids_col[base - 8 : base, :] = tail_in[m // 2, 8:16, :]
-
-            @pl.when(z == 0)
-            def _():
-                prev[base - 8 : base, :] = jnp.zeros((8, hb), F32)
-                ids_col[base - 8 : base, :] = jnp.full((8, hb), -1.0, F32)
-
-    for g in range(GATES):
+            tail_src[o : o + 1, :] = prev[base + T - 1 : base + T, :]
+            tail_src[8 + o : 9 + o, :] = ids_col[base + T - 1 : base + T, :]
+
+    send_if(z < nz - 1, tail_src, tail_in, e_s, e_r, column((z + 1) % nz))
+
+    for step in range(1, nz):
+        plane, g, found = origin(step)
+        late = found if step == nz - 1 else jnp.logical_and(found, jnp.logical_not(inner))
         for col in range(nr):
-            landed(
-                w_all.at[g * hb : (g + 1) * hb, col * cw : (col + 1) * cw], w_r.at[g * nr + col]
-            )
+            block = piece(g, slice(col * cw, (col + 1) * cw))
+            pl.when(late)(functools.partial(landed, block, w_r.at[g * nr + col]))
+
+    @pl.when(z > 0)
+    def _():
+        landed(tail_in, e_r)
+        for o in range(nr):
+            base = 2 * o * stride + 8
+            prev[base - 1 : base, :] = tail_in[o : o + 1, :]
+            ids_col[base - 1 : base, :] = tail_in[8 + o : 9 + o, :]
+
+    @pl.when(z == 0)
+    def _():
+        for o in range(nr):
+            base = 2 * o * stride + 8
+            prev[base - 1 : base, :] = jnp.zeros((1, hb), F32)
+            ids_col[base - 1 : base, :] = jnp.full((1, hb), -1.0, F32)
+
     landed(rows(x_all, k, T), x_s0)
     for x0 in range(nx):
         for y0 in range(2):
@@ -338,31 +364,36 @@
     for i in range(6):
         st_out[i : i + 1, :] = sums[i]
     st_out[6:8, :] = jnp.zeros((2, hb), F32)
-
-    slot = k * nz + z
-    st_in[slot] = st_out[...]
-
-    def tell(d, _):
-        @pl.when(d != me)
-        def _():
-            send(st_out, st_in.at[slot], t_s.at[d], t_r.at[slot], place(d // nr, d % nr))
-
-        return 0
-
-    lax.fori_loop(0, ns * nr, tell, 0)
-
-    for g in range(GATES):
-        wg_out[g] = lax.dot_general(
-            grads[:, g * hb : (g + 1) * hb], x_all[...], (((0,), (0,)), ((), ())),
+    st_z[z] = st_out[...]
+    for plane in range(nz):
+        send_if(plane != z, st_out, st_z.at[z], t_s.at[plane], t_r.at[z], column(plane))
+
+    def quarter(col):
+        return slice(col * cw, (col + 1) * cw)
+
+    def gate_of(step):
+        g = high * step + (1 - high) * (GATES - 1 - step)
+        return g, (nh * g + k) // per
+
+    for step in range(GATES):
+        g, plane = gate_of(step)
+        block = lax.dot_general(
+            grads[:, pl.ds(pl.multiple_of(g * hb, hb), hb)], x_all[...], (((0,), (0,)), ((), ())),
             preferred_element_type=F32,
-        ).astype(BF16)
-        b = g * nh + k
-        owner, i = b // GATES, b % GATES
+        )
+        wg_own[g] = block
+        wg_out[g] = block.astype(BF16)
+        outward = jnp.logical_and(inner, plane == end)
+        inward = jnp.logical_and(jnp.logical_not(inner), plane != z)
         for col in range(nr):
-            here = jnp.logical_and(owner == s, r == col)
-            send_or_local(
-                wg_out.at[g, :, col * cw : (col + 1) * cw], wg_in.at[z * GATES + i],
-                g_s.at[g * nr + col], g_r.at[z * GATES + i], place(owner, col), here,
+            part = wg_out.at[g, :, quarter(col)]
+            send_if(
+                inward, part, wg_end.at[g, :, quarter(col)], g_s.at[step * nr + col],
+                g_e.at[g * nr + col], column(high + half - 1),
+            )
+            send_if(
+                outward, part, wg_mid.at[0, :, quarter(col)], g_s.at[step * nr + col],
+                g_m.at[col], column(end),
             )
 
     chips = [(x0, y0) for x0 in range(nx) for y0 in range(2)]
@@ -385,20 +416,69 @@
         )
 
     scale = 1.0 / math.sqrt(ns * nr * T)
-
-    def heard(d, _):
-        @pl.when(d != slot)
+    for plane in range(nz):
+        pl.when(plane != z)(functools.partial(landed, st_z.at[plane], t_r.at[plane]))
+    total = st_z[0]
+    for plane in range(1, nz):
+        total = total + st_z[plane]
+    st_sum[...] = total * scale
+    st_all[k] = st_sum[...]
+    for j in range(nh):
+        send_if(j != k, st_sum, st_all.at[k], u_s.at[j], u_r.at[k], at(z, j))
+
+    for step in range(GATES):
+        g, plane = gate_of(step)
+        passed = jnp.logical_and(inner, jnp.logical_and(plane != z, plane != end))
+        far = (plane // half != high) & ((plane == 0) | (plane == nz - 1))
+        for col in range(nr):
+            cols = quarter(col)
+
+            @pl.when(passed)
+            def _():
+                landed(wg_end.at[g, :, cols], g_e.at[g * nr + col])
+                wg_out[g, :, cols] = (wg_own[g, :, cols] + wg_end[g, :, cols].astype(F32)).astype(BF16)
+
+            for slot, there in enumerate((jnp.logical_not(far), far)):
+                send_if(
+                    jnp.logical_and(passed, there), wg_out.at[g, :, cols], wg_mid.at[slot, :, cols],
+                    g_s.at[step * nr + col], g_m.at[slot * nr + col], column(plane),
+                )
+
+    _, g, found = origin(0)
+    b = nh * g + k
+    owner, i = b // GATES, b % GATES
+    for col in range(nr):
+        cols = quarter(col)
+
+        @pl.when(found)
         def _():
-            landed(st_in.at[d], t_r.at[d])
-
-        return 0
-
-    lax.fori_loop(0, ns * nr, heard, 0)
+            landed(wg_mid.at[0, :, cols], g_m.at[col])
+            wg_fin[:, cols] = wg_own[g, :, cols] + wg_mid[0, :, cols].astype(F32)
+
+        @pl.when(jnp.logical_and(found, inner))
+        def _():
+            landed(wg_end.at[g, :, cols], g_e.at[g * nr + col])
+            wg_out[g, :, cols] = (wg_fin[:, cols] + wg_end[g, :, cols].astype(F32)).astype(BF16)
+
+        @pl.when(jnp.logical_and(found, jnp.logical_not(inner)))
+        def _():
+            landed(wg_mid.at[1, :, cols], g_m.at[nr + col])
+            wg_out[g, :, cols] = (wg_fin[:, cols] + wg_mid[1, :, cols].astype(F32)).astype(BF16)
+
+        here = jnp.logical_and(owner == s, r == col)
+
+        @pl.when(jnp.logical_and(found, here))
+        def _():
+            local(wg_out.at[g, :, cols], wg_in.at[i], g_r.at[i])
+
+        send_if(
+            jnp.logical_and(found, jnp.logical_not(here)), wg_out.at[g, :, cols], wg_in.at[i],
+            g_f.at[col], g_r.at[i], place(owner, col),
+        )
+
     for j in range(nh):
-        total = st_in[j * nz]
-        for other in range(1, nz):
-            total = total + st_in[j * nz + other]
-        out_p[:, j * hb : (j + 1) * hb] = total[:6] * scale
+        pl.when(j != k)(functools.partial(landed, st_all.at[j], u_r.at[j]))
+        out_p[:, j * hb : (j + 1) * hb] = st_all[j, :6, :]
 
     total = None
     for n in range(len(chips)):
@@ -408,21 +488,9 @@
     out_in[...] = total.astype(BF16)
 
     for i in range(GATES):
-        total = None
-        for other in range(nz):
-            landed(wg_in.at[other * GATES + i], g_r.at[other * GATES + i])
-            term = wg_in[other * GATES + i].astype(F32)
-            total = term if total is None else total + term
-        out_w[i * hb : (i + 1) * hb, :] = total * scale
-
-    def told(d, _):
-        @pl.when(d != me)
-        def _():
-            landed(st_out, t_s.at[d])
-
-        return 0
-
-    lax.fori_loop(0, ns * nr, told, 0)
+        landed(wg_in.at[i], g_r.at[i])
+        out_w[i * hb : (i + 1) * hb, :] = wg_in[i].astype(F32) * scale
+
     for sent, src, sem in unsent:
         if sent is True:
             landed(src, sem)
@@ -454,8 +522,8 @@
         vm((nh, T, 2 * hb), BF16),
         vm((8, T), F32),
         vm((nh, 8, T), F32),
-        vm((nh, 16, hb), F32),
-        vm((nr, 16, hb), F32),
+        vm((16, hb), F32),
+        vm((16, hb), F32),
         vm((L, DI), BF16),
         vm((GATES * hb, DI), BF16),
         vm((L + 8 * nh, hb), F32),
@@ -479,15 +547,21 @@
         vm((nr, T, DI), F32),
         vm((nr, T, DI), BF16),
         vm((nr, T, DI), BF16),
+        vm((GATES, hb, DI), F32),
         vm((GATES, hb, DI), BF16),
-        vm((nz * GATES, hb, cw), BF16),
+        vm((GATES, hb, DI), BF16),
+        vm((2, hb, DI), BF16),
+        vm((hb, DI), F32),
+        vm((GATES, hb, cw), BF16),
         vm((8, hb), F32),
-        vm((ns * nr, 8, hb), F32),
+        vm((nz, 8, hb), F32),
+        vm((8, hb), F32),
+        vm((nh, 8, hb), F32),
     ]
     dma = pltpu.SemaphoreType.DMA
     counts = [
-        None, nr * nx, nr, nr, nh, GATES * nz, GATES * nr, nh, nh, nh, nh, nh, nr, nz, nz, nr, nr, nr, nr,
-        GATES * nr, GATES * nz, ns * nr, ns * nr,
+        None, nr * nx, nr, nr, nh, GATES, nz * nr, GATES * nr, nh, nh, nh, nh, None, None, nz, nz,
+        nr, nr, nr, nr, GATES * nr, GATES * nr, 2 * nr, nr, GATES, nz, nz, nh, nh,
     ]
     sems = [dma if n is None else dma((n,)) for n in counts]
     whole = pl.BlockSpec(memory_space=pltpu.VMEM)

time: 69.2 us -> 63.4 us (0.916)
  the two profiles are of different devices: /device:TPU:27 before, /device:TPU:3 now
where the time goes in v2:
time: 63.4 us; the launch traced here: 63.3 us
  Pallas kernels  62.6 us (99%)
  between operations  0.64 us (1%)
    pallas_call x1, Pallas kernels, by_hidden(): pl.pallas_call(functools.partial(kernel, ns, nr), out_shape=(pltpu.VMEM((...  61.8 us

profile of v2, /device:TPU:3, one launch (start us, length us, event | category | flops | bytes accessed | tf_op | source)
XLA Modules:
  0.0 63.3 jit_solution(14054666734873240629)
XLA Ops:
  0.6 61.8 %shard_map.94 = (bf16[128,1024]{1,0:T(8,128)(2,1)S(1)}, f32[384,256]{1,0:T(8,128)S(1)}, f32[6,1024]{1,0:T(8,128)S(1)}) custom-call(bf16[128,1024]{1,0:T(8,128)(2,1)} %bitcast.5, bf16[384,256]{1,0:T(8,128)(2,1)} %weight.1, f32[128,1024]{1,0:T(8,128)} %bitcast.4, s32[1,128]{1,0:T(1,128)} %ids.1, f32[3,1024]{1,0:T(4,128)} %recur.1, f32[3,1024]{1,0:T(4,128)} %bias.1, ...), custom_call_target="tpu_custom_call" | custom-call | tf_op jit(solution)/shard_map/pallas_call | solution.py:568
  62.4 0.9 %shard_map.95 = (bf16[128,1024]{1,0:T(8,128)(2,1)}, f32[384,256]{1,0:T(8,128)}, f32[6,1024]{1,0:T(8,128)}) custom-call(bf16[128,1024]{1,0:T(8,128)(2,1)S(1)} %get-tuple-element.9.in_a, f32[384,256]{1,0:T(8,128)S(1)} %get-tuple-element.10.in_b, f32[6,1024]{1,0:T(8,128)S(1)} %get-tuple-element.11.in_c), custom_call_target="tpu_custom_call" | custom-call | tf_op jit(solution)/shard_map/pallas_call | solution.py:583

commit v3 on v2

--- a/solution.py
+++ b/solution.py
@@ -91,22 +91,24 @@
 
 
 def kernel(
-    ns, nr, feats, weight, states, ids, recur, bias, upstream,
+    ns, nr, feats_hbm, weight_hbm, states_hbm, ids_hbm, recur_hbm, bias_hbm, upstream_hbm,
     out_in, out_w, out_p,
-    pay_src, pay, ids_src, ids_all, tail_src, tail_in, x_all, w_all, prev, ids_col, up, jac,
-    co_z, co_r, co_c, rprior, prior_all,
+    weight, states, ids, recur, bias, upstream,
+    pay_src, pay, up_in, ids_src, ids_all, tail_src, tail_mid, tail_in, x_all, w_all, prev, ids_col, same_all, up,
+    jac, co_z, co_r, co_c, rprior, prior_all,
     scan_a, scan_b, carry, seg_out, seg_in, lam, grads, part_out, part_in, part_keep, fin_out, fin_in,
     wg_own, wg_out, wg_end, wg_mid, wg_fin, wg_in, st_out, st_z, st_sum, st_all,
-    x_s0, x_sx, x_sy, x_sd, x_r, w_s, w_f, w_r, p_s, p_r, i_s, i_r, e_s, e_r, c_s, c_r, d_s, d_r, f_s, f_r,
-    g_s, g_e, g_m, g_f, g_r, t_s, t_r, u_s, u_r,
+    l_s, x_sx, x_sy, x_sd, x_r, w_s, w_f, w_r, p_s, p_r, v_s, v_r, i_s, i_r, e_s, e_r, n_s, n_r, c_s, c_r,
+    d_s, d_r, f_s, f_r, g_s, g_e, g_m, g_f, g_r, t_s, t_r, u_s, u_r,
 ):
-    T, DI = feats.shape
+    T, DI = feats_hbm.shape
     H = states.shape[1]
     nh, nz, nx = 2 * nr, ns // 2, nr // 2
     hb, cw = H // nh, DI // nr
     s, r = lax.axis_index("seq"), lax.axis_index("rep")
     z, y, x, c = s // 2, s % 2, r // 2, r % 2
-    k = 2 * r + y
+    q = 2 * r + y
+    k = nx * 2 * c + 2 * x + y
     half, per = nz // 2, GATES * nh // nz
     high = z // half
     inner = jnp.logical_or(z == half - 1, z == half)
@@ -117,7 +119,7 @@
         return {"seq": a, "rep": b}
 
     def at(plane, j):
-        return place(2 * plane + j % 2, j // 2)
+        return place(2 * plane + j % 2, 2 * (j // 2 % nx) + j // (2 * nx))
 
     def column(plane):
         return place(2 * plane + y, r)
@@ -160,12 +162,31 @@
         pl.when(j != k)(functools.partial(greet, at(z, j)))
     for plane in range(nz):
         pl.when(plane != z)(functools.partial(greet, column(plane)))
+    loads = [
+        (weight_hbm, weight), (feats_hbm, rows(x_all, q, T)), (states_hbm, states), (ids_hbm, ids),
+        (upstream_hbm, upstream), (recur_hbm, recur), (bias_hbm, bias),
+    ]
+    for n, (src, dst) in enumerate(loads):
+        local(src, dst, l_s.at[n])
+
+    def loaded(n):
+        landed(loads[n][1], l_s.at[n])
+
+    loaded(2)
+    loaded(3)
     for j in range(nh):
-        pay_src[j, :, :hb] = states[:, j * hb : (j + 1) * hb].astype(BF16)
-        pay_src[j, :, hb:] = upstream[:, j * hb : (j + 1) * hb]
+        pay_src[j] = states[:, j * hb : (j + 1) * hb].astype(BF16)
+    tail_src[0:4, :] = jnp.broadcast_to(states[T - 1 : T, :], (4, H))
+    tail_src[4:8, :] = jnp.broadcast_to(ids[0:1, T - 1 : T].astype(F32), (4, H))
     ids_src[...] = jnp.broadcast_to(ids[...].astype(F32), ids_src.shape)
-
+    loaded(0)
+    loaded(1)
+    loaded(4)
     pl.semaphore_wait(barrier, nh - 1 + nz - 1)
+
+    hands_on = jnp.logical_and(y == 1, z < nz - 1)
+    takes_over = jnp.logical_and(y == 1, z > 0)
+    send_if(hands_on, tail_src, tail_mid, n_s, n_r, column((z + 1) % nz))
 
     def piece(g, col):
         return w_all.at[pl.ds(pl.multiple_of(g * hb, hb), hb), col]
@@ -179,7 +200,6 @@
             at(z, j), j == k,
         )
     partner = place(s, r + 1 - 2 * c)
-    local(feats, rows(x_all, k, T), x_s0)
 
     def share(step, src, dx, dy):
         x0, y0 = (x + dx) % nx, (y + dy) % 2
@@ -199,60 +219,96 @@
                 send_if(allowed, src, dst, x_sy.at[step], x_r.at[slot], place(2 * z + 1 - y, r))
         send_if(True, src, dst, x_sd.at[step], x_r.at[slot], partner)
 
-    share(0, feats, 0, 0)
-
+    share(0, None, 0, 0)
+    pl.when(takes_over)(functools.partial(landed, tail_mid, n_r))
     for j in range(nh):
-        send_or_local(ids_src, ids_all.at[k], i_s.at[j], i_r.at[k], at(z, j), k == j)
-        send_or_local(pay_src.at[j], pay.at[k], p_s.at[j], p_r.at[k], at(z, j), k == j)
+        part = tail_mid.at[:, j * hb : (j + 1) * hb]
+        send_if(jnp.logical_and(takes_over, j != k), part, tail_in.at[r], e_s.at[j], e_r.at[r], at(z, j))
+
+        @pl.when(jnp.logical_and(takes_over, j == k))
+        def _():
+            local(part, tail_in.at[r], e_r.at[r])
+
+    for j in range(nh):
+        send_or_local(ids_src, ids_all.at[q], i_s.at[j], i_r.at[q], at(z, j), k == j)
+        send_or_local(pay_src.at[j], pay.at[q], p_s.at[j], p_r.at[q], at(z, j), k == j)
 
     def origin(step):
         plane = (z + (1 - 2 * high) * step + nz) % nz
         g = (per * plane - k + nh - 1) // nh
         return plane, g % GATES, jnp.logical_and(g < GATES, nh * g + k < per * (plane + 1))
 
+    order = []
+    for n in range(nr):
+        chip = (x + n // 2) % nx
+        order.append(2 * chip + (c + n) % 2)
+
     def spread(step):
         plane, g, found = origin(step)
-        for col in range(nr):
-            cols = slice(col * cw, (col + 1) * cw)
-            block, sem = piece(g, cols), w_r.at[g * nr + col]
+        for n, col in enumerate(order):
+            block = piece(g, pl.ds(pl.multiple_of(col * cw, cw), cw))
+            sem = w_r.at[g * nr + col]
             if step == 0:
                 pl.when(found)(functools.partial(landed, block, sem))
-                for n, target in enumerate((half - high, z + 1 - 2 * (z % half))):
-                    send_if(found, block, block, w_f.at[n * nr + col], sem, column(target))
+                for i, target in enumerate((half - high, z + 1 - 2 * (z % half))):
+                    send_if(found, block, block, w_f.at[i * nr + n], sem, column(target))
             else:
                 go = jnp.logical_and(found, inner)
                 pl.when(go)(functools.partial(landed, block, sem))
-                send_if(go, block, block, w_f.at[(step + 1) * nr + col], sem, column(end))
+                send_if(go, block, block, w_f.at[(step + 1) * nr + n], sem, column(end))
 
     hops = [(dx, dy) for dx in range(nx) for dy in range(2)]
     hops.sort(key=lambda hop: (hop[0] > 0) + hop[1])
+
+    def relay(step):
+        dx, dy = hops[step]
+        slot = 2 * (2 * ((x + dx) % nx) + c) + (y + dy) % 2
+        landed(rows(x_all, slot, T), x_r.at[slot])
+        share(step, None, dx, dy)
+
     spread(0)
     spread(1)
-    for step, (dx, dy) in enumerate(hops):
-        if step > 0:
-            slot = 2 * (2 * ((x + dx) % nx) + c) + (y + dy) % 2
-            landed(rows(x_all, slot, T), x_r.at[slot])
-            share(step, None, dx, dy)
+    for step in range(1, len(hops) - 1):
+        relay(step)
+    for j in range(nh):
+        part = upstream.at[:, j * hb : (j + 1) * hb]
+        send_or_local(part, up_in.at[q], v_s.at[j], v_r.at[q], at(z, j), k == j)
     spread(2)
 
     stride = T + 8
     for m in range(nh):
         base = m * stride + 8
+        span = slice(m * T, (m + 1) * T)
         landed(ids_all.at[m], i_r.at[m])
         landed(pay.at[m], p_r.at[m])
-        prev[base : base + T, :] = pay[m, :, :hb].astype(F32)
-        up[m * T : (m + 1) * T, :] = pay[m, :, hb:].astype(F32)
+        prev[base : base + T, :] = pay[m].astype(F32)
         ids_col[base : base + T, :] = jnp.broadcast_to(ids_all[m, 0:1, :], (hb, T)).T
         if m % 2:
-            before = base - stride + T
-            o = m // 2
-            prev[base - 8 : base, :] = prev[before - 8 : before, :]
-            ids_col[base - 8 : base, :] = ids_col[before - 8 : before, :]
-            tail_src[o : o + 1, :] = prev[base + T - 1 : base + T, :]
-            tail_src[8 + o : 9 + o, :] = ids_col[base + T - 1 : base + T, :]
-
-    send_if(z < nz - 1, tail_src, tail_in, e_s, e_r, column((z + 1) % nz))
-
+            before = base - stride + T - 1
+            prev[base - 1 : base, :] = prev[before : before + 1, :]
+            ids_col[base - 1 : base, :] = ids_col[before : before + 1, :]
+        else:
+
+            @pl.when(z > 0)
+            def _():
+                landed(tail_in.at[m // 2], e_r.at[m // 2])
+                prev[base - 1 : base, :] = tail_in[m // 2, 0:1, :]
+                ids_col[base - 1 : base, :] = tail_in[m // 2, 4:5, :]
+
+            @pl.when(z == 0)
+            def _():
+                prev[base - 1 : base, :] = jnp.zeros((1, hb), F32)
+                ids_col[base - 1 : base, :] = jnp.full((1, hb), -1.0, F32)
+
+        same = jnp.where(
+            ids_col[base : base + T, :] == ids_col[base - 1 : base - 1 + T, :], 1.0, 0.0
+        )
+        same_all[span, :] = same
+        prior_all[span, :] = prev[base - 1 : base - 1 + T, :] * same
+
+    loaded(5)
+    loaded(6)
+    relay(len(hops) - 1)
     for step in range(1, nz):
         plane, g, found = origin(step)
         late = found if step == nz - 1 else jnp.logical_and(found, jnp.logical_not(inner))
@@ -260,54 +316,36 @@
             block = piece(g, slice(col * cw, (col + 1) * cw))
             pl.when(late)(functools.partial(landed, block, w_r.at[g * nr + col]))
 
-    @pl.when(z > 0)
-    def _():
-        landed(tail_in, e_r)
-        for o in range(nr):
-            base = 2 * o * stride + 8
-            prev[base - 1 : base, :] = tail_in[o : o + 1, :]
-            ids_col[base - 1 : base, :] = tail_in[8 + o : 9 + o, :]
-
-    @pl.when(z == 0)
-    def _():
-        for o in range(nr):
-            base = 2 * o * stride + 8
-            prev[base - 1 : base, :] = jnp.zeros((1, hb), F32)
-            ids_col[base - 1 : base, :] = jnp.full((1, hb), -1.0, F32)
-
-    landed(rows(x_all, k, T), x_s0)
-    for x0 in range(nx):
-        for y0 in range(2):
-            slot = 2 * (2 * x0 + 1 - c) + y0
-            landed(rows(x_all, slot, T), x_r.at[slot])
-
     group = pl.ds(pl.multiple_of(k * hb, hb), hb)
     rz, rr, rc = (recur[i : i + 1, group] for i in range(GATES))
     bz, br, bc = (bias[i : i + 1, group] for i in range(GATES))
+    for dx, dy in hops:
+        for core in range(2):
+            m = 2 * (2 * ((x + dx) % nx) + (c + core) % 2) + (y + dy) % 2
+            if core:
+                landed(rows(x_all, m, T), x_r.at[m])
+            span = pl.ds(pl.multiple_of(m * T, T), T)
+            pre = lax.dot_general(
+                x_all[span, :], w_all[...], (((1,), (1,)), ((), ())), preferred_element_type=F32
+            )
+            prior = prior_all[span, :]
+            gz = jax.nn.sigmoid(pre[:, :hb] + rz * prior + bz)
+            gr = jax.nn.sigmoid(pre[:, hb : 2 * hb] + rr * prior + br)
+            rp = gr * prior
+            gc = jnp.tanh(pre[:, 2 * hb :] + rc * rp + bc)
+            az = (gc - prior) * gz * (1.0 - gz)
+            ac = gz * (1.0 - gc * gc)
+            slope = rp * (1.0 - gr)
+            acr = ac * rc
+            co_z[span, :] = az
+            co_c[span, :] = ac
+            co_r[span, :] = acr * slope
+            rprior[span, :] = rp
+            jac[span, :] = same_all[span, :] * (1.0 - gz + az * rz + acr * (gr + slope * rr))
+
     for m in range(nh):
-        span = slice(m * T, (m + 1) * T)
-        base = m * stride + 8
-        pre = lax.dot_general(
-            x_all[span, :], w_all[...], (((1,), (1,)), ((), ())), preferred_element_type=F32
-        )
-        same = jnp.where(
-            ids_col[base : base + T, :] == ids_col[base - 1 : base - 1 + T, :], 1.0, 0.0
-        )
-        prior = prev[base - 1 : base - 1 + T, :] * same
-        gz = jax.nn.sigmoid(pre[:, :hb] + rz * prior + bz)
-        gr = jax.nn.sigmoid(pre[:, hb : 2 * hb] + rr * prior + br)
-        rp = gr * prior
-        gc = jnp.tanh(pre[:, 2 * hb :] + rc * rp + bc)
-        az = (gc - prior) * gz * (1.0 - gz)
-        ac = gz * (1.0 - gc * gc)
-        slope = rp * (1.0 - gr)
-        acr = ac * rc
-        co_z[span, :] = az
-        co_c[span, :] = ac
-        co_r[span, :] = acr * slope
-        rprior[span, :] = rp
-        prior_all[span, :] = prior
-        jac[span, :] = same * (1.0 - gz + az * rz + acr * (gr + slope * rr))
+        landed(up_in.at[m], v_r.at[m])
+        up[m * T : (m + 1) * T, :] = up_in[m].astype(F32)
 
     def back(i, state):
         a, b = state
@@ -396,24 +434,28 @@
                 g_m.at[col], column(end),
             )
 
-    chips = [(x0, y0) for x0 in range(nx) for y0 in range(2)]
-    for n, (x0, y0) in enumerate(chips):
-        part_out[n] = jnp.dot(
-            rows(grads, 2 * (2 * x0 + 1 - c) + y0, T)[...], w_all[...], preferred_element_type=F32
-        ).astype(BF16)
+    chips = [(x + 1, y + 1), (x + 1, y), (x, y + 1), (x, y)]
+
+    def tokens(n, core):
+        return rows(grads, 2 * (2 * (chips[n][0] % nx) + core) + chips[n][1] % 2, T)[...]
+
+    for n in range(len(chips)):
+        part_out[n] = jnp.dot(tokens(n, 1 - c), w_all[...], preferred_element_type=F32).astype(BF16)
         send_if(True, part_out.at[n], part_in.at[n], d_s.at[n], d_r.at[n], partner)
-    for n, (x0, y0) in enumerate(chips):
-        part_keep[n] = jnp.dot(
-            rows(grads, 2 * (2 * x0 + c) + y0, T)[...], w_all[...], preferred_element_type=F32
-        )
-    chip = 2 * x + y
-    for n, (x0, y0) in enumerate(chips):
+    for n in range(len(chips)):
+        part_keep[n] = jnp.dot(tokens(n, c), w_all[...], preferred_element_type=F32)
+
+    first = place(2 * z + (y + c) % 2, 2 * ((x + 1 - c) % nx) + c)
+    second = place(2 * z + (y + 1 - c) % 2, 2 * ((x + c) % nx) + c)
+
+    def both(n):
         landed(part_in.at[n], d_r.at[n])
-        fin_out[n] = (part_keep[n] + part_in[n].astype(F32)).astype(BF16)
-        send_or_local(
-            fin_out.at[n], fin_in.at[chip], f_s.at[n], f_r.at[chip],
-            place(2 * z + y0, 2 * x0 + c), chip == n,
-        )
+        return part_keep[n] + part_in[n].astype(F32)
+
+    fin_out[0] = both(0).astype(BF16)
+    send_if(True, fin_out.at[0], fin_in.at[0], f_s.at[0], f_r.at[0], first)
+    fin_out[1] = both(1 + c).astype(BF16)
+    send_if(True, fin_out.at[1], fin_in.at[1], f_s.at[1], f_r.at[1], first)
 
     scale = 1.0 / math.sqrt(ns * nr * T)
     for plane in range(nz):
@@ -426,7 +468,15 @@
     for j in range(nh):
         send_if(j != k, st_sum, st_all.at[k], u_s.at[j], u_r.at[k], at(z, j))
 
+    def turn():
+        total = both(2 - c)
+        landed(fin_in.at[0], f_r.at[0])
+        fin_out[2] = (total + fin_in[0].astype(F32)).astype(BF16)
+        send_if(True, fin_out.at[2], fin_in.at[2], f_s.at[2], f_r.at[2], second)
+
     for step in range(GATES):
+        if step == 1:
+            turn()
         g, plane = gate_of(step)
         passed = jnp.logical_and(inner, jnp.logical_and(plane != z, plane != end))
         far = (plane // half != high) & ((plane == 0) | (plane == nz - 1))
@@ -480,11 +530,10 @@
         pl.when(j != k)(functools.partial(landed, st_all.at[j], u_r.at[j]))
         out_p[:, j * hb : (j + 1) * hb] = st_all[j, :6, :]
 
-    total = None
-    for n in range(len(chips)):
+    total = both(3)
+    for n in (1, 2):
         landed(fin_in.at[n], f_r.at[n])
-        term = fin_in[n].astype(F32)
-        total = term if total is None else total + term
+        total = total + fin_in[n].astype(F32)
     out_in[...] = total.astype(BF16)
 
     for i in range(GATES):
@@ -518,16 +567,25 @@
     L = nh * T
     vm = pltpu.VMEM
     scratch = [
-        vm((nh, T, 2 * hb), BF16),
-        vm((nh, T, 2 * hb), BF16),
+        vm(weight_t.shape, BF16),
+        vm((T, H), F32),
+        vm((1, T), jnp.int32),
+        vm((GATES, H), F32),
+        vm((GATES, H), F32),
+        vm((T, H), BF16),
+        vm((nh, T, hb), BF16),
+        vm((nh, T, hb), BF16),
+        vm((nh, T, hb), BF16),
         vm((8, T), F32),
         vm((nh, 8, T), F32),
-        vm((16, hb), F32),
-        vm((16, hb), F32),
+        vm((8, H), F32),
+        vm((8, H), F32),
+        vm((nr, 8, hb), F32),
         vm((L, DI), BF16),
         vm((GATES * hb, DI), BF16),
         vm((L + 8 * nh, hb), F32),
         vm((L + 8 * nh, hb), F32),
+        vm((L, hb), F32),
         vm((L, hb), F32),
         vm((L, hb), F32),
         vm((L, hb), F32),
@@ -545,8 +603,8 @@
         vm((nr, T, DI), BF16),
         vm((nr, T, DI), BF16),
         vm((nr, T, DI), F32),
-        vm((nr, T, DI), BF16),
-        vm((nr, T, DI), BF16),
+        vm((3, T, DI), BF16),
+        vm((3, T, DI), BF16),
         vm((GATES, hb, DI), F32),
         vm((GATES, hb, DI), BF16),
         vm((GATES, hb, DI), BF16),
@@ -560,8 +618,8 @@
     ]
     dma = pltpu.SemaphoreType.DMA
     counts = [
-        None, nr * nx, nr, nr, nh, GATES, nz * nr, GATES * nr, nh, nh, nh, nh, None, None, nz, nz,
-        nr, nr, nr, nr, GATES * nr, GATES * nr, 2 * nr, nr, GATES, nz, nz, nh, nh,
+        7, nr * nx, nr, nr, nh, GATES, nz * nr, GATES * nr, nh, nh, nh, nh, nh, nh, nh, nr, None, None,
+        nz, nz, nr, nr, 3, 3, GATES * nr, GATES * nr, 2 * nr, nr, GATES, nz, nz, nh, nh,
     ]
     sems = [dma if n is None else dma((n,)) for n in counts]
     whole = pl.BlockSpec(memory_space=pltpu.VMEM)
@@ -572,7 +630,7 @@
             pltpu.VMEM(weight_t.shape, F32),
             pltpu.VMEM((6, H), F32),
         ),
-        in_specs=[whole] * 7,
+        in_specs=[pl.BlockSpec(memory_space=pltpu.HBM)] * 7,
         out_specs=(whole,) * 3,
         scratch_shapes=scratch + sems,
         compiler_params=pltpu.CompilerParams(

time: 63.4 us -> 53.4 us (0.84)
  Pallas kernels: 62.6 us -> 52.6 us
    pallas_call x1, Pallas kernels: 61.8 us -> 51.7 us  [by_hidden(): pl.pallas_call(functools.partial(kernel, ns, nr), out_shape=(pltpu.VMEM((...]
where the time goes in v3:
time: 53.4 us; the launch traced here: 53.2 us
  Pallas kernels  52.6 us (99%)
  between operations  0.64 us (1%)
    pallas_call x1, Pallas kernels, by_hidden(): pl.pallas_call(functools.partial(kernel, ns, nr), out_shape=(pltpu.VMEM((...  51.7 us

profile of v3, /device:TPU:3, one launch (start us, length us, event | category | flops | bytes accessed | tf_op | source)
XLA Modules:
  0.0 53.2 jit_solution(12961289835481956600)
XLA Ops:
  0.6 51.7 %shard_map.94 = (bf16[128,1024]{1,0:T(8,128)(2,1)S(1)}, f32[384,256]{1,0:T(8,128)S(1)}, f32[6,1024]{1,0:T(8,128)S(1)}) custom-call(bf16[128,1024]{1,0:T(8,128)(2,1)} %bitcast.5, bf16[384,256]{1,0:T(8,128)(2,1)} %weight_hbm.1, f32[128,1024]{1,0:T(8,128)} %bitcast.4, s32[1,128]{1,0:T(1,128)} %ids_hbm.1, f32[3,1024]{1,0:T(4,128)} %recur_hbm.1, ...), custom_call_target="tpu_custom_call" | custom-call | tf_op jit(solution)/shard_map/pallas_call | solution.py:626
  52.4 0.9 %shard_map.95 = (bf16[128,1024]{1,0:T(8,128)(2,1)}, f32[384,256]{1,0:T(8,128)}, f32[6,1024]{1,0:T(8,128)}) custom-call(bf16[128,1024]{1,0:T(8,128)(2,1)S(1)} %get-tuple-element.9.in_a, f32[384,256]{1,0:T(8,128)S(1)} %get-tuple-element.10.in_b, f32[6,1024]{1,0:T(8,128)S(1)} %get-tuple-element.11.in_c), custom_call_target="tpu_custom_call" | custom-call | tf_op jit(solution)/shard_map/pallas_call | solution.py:641

commit v4 on v3

--- a/solution.py
+++ b/solution.py
@@ -94,11 +94,11 @@
     ns, nr, feats_hbm, weight_hbm, states_hbm, ids_hbm, recur_hbm, bias_hbm, upstream_hbm,
     out_in, out_w, out_p,
     weight, states, ids, recur, bias, upstream,
-    pay_src, pay, up_in, ids_src, ids_all, tail_src, tail_mid, tail_in, x_all, w_all, prev, ids_col, same_all, up,
-    jac, co_z, co_r, co_c, rprior, prior_all,
+    pay_src, pay, up_in, tail_src, tail_mid, tail_in, x_all, w_all, prev, ids_col, same_all, up,
+    pre, jac, co_z, co_r, co_c, rprior, prior_all,
     scan_a, scan_b, carry, seg_out, seg_in, lam, grads, part_out, part_in, part_keep, fin_out, fin_in,
     wg_own, wg_out, wg_end, wg_mid, wg_fin, wg_in, st_out, st_z, st_sum, st_all,
-    l_s, x_sx, x_sy, x_sd, x_r, w_s, w_f, w_r, p_s, p_r, v_s, v_r, i_s, i_r, e_s, e_r, n_s, n_r, c_s, c_r,
+    l_s, x_s, x_r, w_s, w_f, w_r, p_s, p_r, v_s, v_r, e_s, e_r, n_s, n_r, c_s, c_r,
     d_s, d_r, f_s, f_r, g_s, g_e, g_m, g_f, g_r, t_s, t_r, u_s, u_r,
 ):
     T, DI = feats_hbm.shape
@@ -136,19 +136,12 @@
     def landed(dst, sem):
         pltpu.make_async_copy(dst, dst, sem).wait()
 
-    def send_if(allowed, src, dst, ssem, rsem, where):
-        @pl.when(allowed)
-        def _():
-            send(src, dst, ssem, rsem, where)
-
-        unsent.append((allowed, src, ssem))
+    def send_if(allowed, *args):
+        pl.when(allowed)(functools.partial(send, *args))
 
     def send_or_local(src, dst, ssem, rsem, where, here):
         send_if(jnp.logical_not(here), src, dst, ssem, rsem, where)
-
-        @pl.when(here)
-        def _():
-            local(src, dst, rsem)
+        pl.when(here)(functools.partial(local, src, dst, rsem))
 
     def rows(ref, block, count):
         return ref.at[pl.ds(pl.multiple_of(block * count, count), count), :]
@@ -172,66 +165,51 @@
     def loaded(n):
         landed(loads[n][1], l_s.at[n])
 
-    loaded(2)
-    loaded(3)
-    for j in range(nh):
-        pay_src[j] = states[:, j * hb : (j + 1) * hb].astype(BF16)
-    tail_src[0:4, :] = jnp.broadcast_to(states[T - 1 : T, :], (4, H))
-    tail_src[4:8, :] = jnp.broadcast_to(ids[0:1, T - 1 : T].astype(F32), (4, H))
-    ids_src[...] = jnp.broadcast_to(ids[...].astype(F32), ids_src.shape)
-    loaded(0)
-    loaded(1)
-    loaded(4)
-    pl.semaphore_wait(barrier, nh - 1 + nz - 1)
-
-    hands_on = jnp.logical_and(y == 1, z < nz - 1)
-    takes_over = jnp.logical_and(y == 1, z > 0)
-    send_if(hands_on, tail_src, tail_mid, n_s, n_r, column((z + 1) % nz))
-
     def piece(g, col):
         return w_all.at[pl.ds(pl.multiple_of(g * hb, hb), hb), col]
+
+    loaded(0)
+    pl.semaphore_wait(barrier, nh - 1 + nz - 1)
 
     mine = pl.ds(pl.multiple_of(r * cw, cw), cw)
     for i in range(GATES):
         b = GATES * s + i
         g, j = b // nh, b % nh
-        send_or_local(
-            weight.at[i * hb : (i + 1) * hb, :], piece(g, mine), w_s.at[i], w_r.at[g * nr + r],
-            at(z, j), j == k,
-        )
+        part = weight.at[i * hb : (i + 1) * hb, :]
+        send_or_local(part, piece(g, mine), w_s.at[i], w_r.at[g * nr + r], at(z, j), j == k)
+        unsent.append((j != k, part, w_s.at[i]))
+
     partner = place(s, r + 1 - 2 * c)
-
-    def share(step, src, dx, dy):
-        x0, y0 = (x + dx) % nx, (y + dy) % 2
-        slot = 2 * (2 * x0 + c) + y0
-        dst = rows(x_all, slot, T)
-        src = dst if src is None else src
-        if dy == 0 or dx == 0:
-            for other in range(1, nx):
-                if dx == 0:
-                    allowed = True if dy == 0 else c == 0
-                    send_if(
-                        allowed, src, dst, x_sx.at[step * nx + other], x_r.at[slot],
-                        place(s, 2 * ((x + other) % nx) + c),
-                    )
-            if dy == 0:
-                allowed = True if dx == 0 else c == 1
-                send_if(allowed, src, dst, x_sy.at[step], x_r.at[slot], place(2 * z + 1 - y, r))
-        send_if(True, src, dst, x_sd.at[step], x_r.at[slot], partner)
-
-    share(0, None, 0, 0)
-    pl.when(takes_over)(functools.partial(landed, tail_mid, n_r))
+    nearest = place(2 * z + (y + c) % 2, 2 * ((x + 1 - c) % nx) + c)
+    across = place(2 * z + (y + 1 - c) % 2, 2 * ((x + c) % nx) + c)
+
+    def features(dx, dy, core):
+        return 2 * (2 * ((x + dx) % nx) + (c + core) % 2) + (y + dy) % 2
+
+    def share(dx, dy, targets):
+        slot = features(dx, dy, 0)
+        block = rows(x_all, slot, T)
+        for where in targets:
+            send(block, block, x_s, x_r.at[slot], where)
+
+    loaded(1)
+    share(0, 0, (nearest, across, partner))
+    unsent.append((True, x_all.at[0 : (nh - 1) * T, :], x_s))
+
+    loaded(2)
+    loaded(3)
+    tail_src[0:4, :] = jnp.broadcast_to(states[T - 1 : T, :], (4, H))
+    tail_src[4:8, :] = jnp.broadcast_to(ids[0:1, T - 1 : T].astype(F32), (4, H))
+    hands_on = jnp.logical_and(y == 1, z < nz - 1)
+    takes_over = jnp.logical_and(y == 1, z > 0)
+    send_if(hands_on, tail_src, tail_mid, n_s, n_r, column((z + 1) % nz))
+    unsent.append((hands_on, tail_src, n_s))
     for j in range(nh):
-        part = tail_mid.at[:, j * hb : (j + 1) * hb]
-        send_if(jnp.logical_and(takes_over, j != k), part, tail_in.at[r], e_s.at[j], e_r.at[r], at(z, j))
-
-        @pl.when(jnp.logical_and(takes_over, j == k))
-        def _():
-            local(part, tail_in.at[r], e_r.at[r])
-
+        pay_src[j, 0:T, :] = states[:, j * hb : (j + 1) * hb].astype(BF16)
+        pay_src[j, T:, :] = jnp.broadcast_to(ids[...].astype(F32), (16, hb)).astype(BF16)
     for j in range(nh):
-        send_or_local(ids_src, ids_all.at[q], i_s.at[j], i_r.at[q], at(z, j), k == j)
-        send_or_local(pay_src.at[j], pay.at[q], p_s.at[j], p_r.at[q], at(z, j), k == j)
+        send_or_local(pay_src.at[j], pay.at[q], p_s, p_r, at(z, j), k == j)
+    unsent.append((True, pay.at[0 : nh - 1], p_s))
 
     def origin(step):
         plane = (z + (1 - 2 * high) * step + nz) % nz
@@ -243,46 +221,62 @@
         chip = (x + n // 2) % nx
         order.append(2 * chip + (c + n) % 2)
 
-    def spread(step):
+    def spread(step, numbers):
         plane, g, found = origin(step)
-        for n, col in enumerate(order):
-            block = piece(g, pl.ds(pl.multiple_of(col * cw, cw), cw))
-            sem = w_r.at[g * nr + col]
+        outer = jnp.logical_and(found, jnp.logical_not(inner))
+        within = jnp.logical_and(found, inner)
+        far, near = column(half - high), column(z + 1 - 2 * (z % half))
+        for n in numbers:
+            block = piece(g, pl.ds(pl.multiple_of(order[n] * cw, cw), cw))
+            sem = w_r.at[g * nr + order[n]]
             if step == 0:
                 pl.when(found)(functools.partial(landed, block, sem))
-                for i, target in enumerate((half - high, z + 1 - 2 * (z % half))):
-                    send_if(found, block, block, w_f.at[i * nr + n], sem, column(target))
+                send_if(found, block, block, w_f.at[0], sem, far)
+                send_if(within, block, block, w_f.at[0], sem, near)
             else:
-                go = jnp.logical_and(found, inner)
-                pl.when(go)(functools.partial(landed, block, sem))
-                send_if(go, block, block, w_f.at[(step + 1) * nr + n], sem, column(end))
-
-    hops = [(dx, dy) for dx in range(nx) for dy in range(2)]
-    hops.sort(key=lambda hop: (hop[0] > 0) + hop[1])
-
-    def relay(step):
-        dx, dy = hops[step]
-        slot = 2 * (2 * ((x + dx) % nx) + c) + (y + dy) % 2
+                pl.when(within)(functools.partial(landed, block, sem))
+                send_if(within, block, block, w_f.at[step], sem, column(end))
+        if step == 0:
+            for n in numbers:
+                block = piece(g, pl.ds(pl.multiple_of(order[n] * cw, cw), cw))
+                send_if(outer, block, block, w_f.at[0], w_r.at[g * nr + order[n]], near)
+            unsent.append((found, w_all.at[0 : 2 * hb, :], w_f.at[0]))
+        elif numbers[-1] == nr - 1:
+            unsent.append((within, w_all.at[0:hb, :], w_f.at[step]))
+
+    def relay(dx, dy, targets):
+        slot = features(dx, dy, 0)
         landed(rows(x_all, slot, T), x_r.at[slot])
-        share(step, None, dx, dy)
-
-    spread(0)
-    spread(1)
-    for step in range(1, len(hops) - 1):
-        relay(step)
+        share(dx, dy, targets)
+
+    spread(0, range(nr))
+    pl.when(takes_over)(functools.partial(landed, tail_mid, n_r))
+    for j in range(nh):
+        part = tail_mid.at[:, j * hb : (j + 1) * hb]
+        here = j == k
+        send_if(jnp.logical_and(takes_over, j != k), part, tail_in.at[r], e_s, e_r, at(z, j))
+        pl.when(jnp.logical_and(takes_over, here))(functools.partial(local, part, tail_in.at[r], e_r))
+    unsent.append((takes_over, st_all.at[0 : nh - 1], e_s))
+    spread(1, range(nr // 2))
+    relay(c, 1 - c, (nearest, partner))
+    spread(1, range(nr // 2, nr))
+    relay(1 - c, c, (partner,))
+    loaded(4)
     for j in range(nh):
         part = upstream.at[:, j * hb : (j + 1) * hb]
-        send_or_local(part, up_in.at[q], v_s.at[j], v_r.at[q], at(z, j), k == j)
-    spread(2)
+        send_or_local(part, up_in.at[q], v_s, v_r, at(z, j), k == j)
+    unsent.append((True, up_in.at[0 : nh - 1], v_s))
+    spread(2, range(nr))
 
     stride = T + 8
+    landed(pay, p_r)
+    pl.when(z > 0)(functools.partial(landed, tail_in, e_r))
     for m in range(nh):
         base = m * stride + 8
         span = slice(m * T, (m + 1) * T)
-        landed(ids_all.at[m], i_r.at[m])
-        landed(pay.at[m], p_r.at[m])
-        prev[base : base + T, :] = pay[m].astype(F32)
-        ids_col[base : base + T, :] = jnp.broadcast_to(ids_all[m, 0:1, :], (hb, T)).T
+        prev[base : base + T, :] = pay[m, 0:T, :].astype(F32)
+        ids_row = pay[m, T:, :].astype(F32)[0:1, :]
+        ids_col[base : base + T, :] = jnp.broadcast_to(ids_row, (hb, T)).T
         if m % 2:
             before = base - stride + T - 1
             prev[base - 1 : base, :] = prev[before : before + 1, :]
@@ -291,7 +285,6 @@
 
             @pl.when(z > 0)
             def _():
-                landed(tail_in.at[m // 2], e_r.at[m // 2])
                 prev[base - 1 : base, :] = tail_in[m // 2, 0:1, :]
                 ids_col[base - 1 : base, :] = tail_in[m // 2, 4:5, :]
 
@@ -308,50 +301,76 @@
 
     loaded(5)
     loaded(6)
-    relay(len(hops) - 1)
-    for step in range(1, nz):
-        plane, g, found = origin(step)
-        late = found if step == nz - 1 else jnp.logical_and(found, jnp.logical_not(inner))
+    (_, g0, found0), (_, g1, _), (_, g2, _), (_, g3, found3) = (origin(step) for step in range(nz))
+    own, wide = found0.astype(jnp.int32), found3.astype(jnp.int32)
+    early = own * g0 + (1 - own) * g1
+    late = wide * g3 + (1 - wide) * g2
+    middle = (GATES - early - late) % GATES
+    outer = jnp.logical_not(inner)
+
+    def arrived(g, unseen):
         for col in range(nr):
             block = piece(g, slice(col * cw, (col + 1) * cw))
-            pl.when(late)(functools.partial(landed, block, w_r.at[g * nr + col]))
+            pl.when(unseen)(functools.partial(landed, block, w_r.at[g * nr + col]))
+
+    def project(span, g):
+        return lax.dot_general(
+            x_all[span, :], piece(g, slice(None))[...], (((1,), (1,)), ((), ())),
+            preferred_element_type=F32,
+        )
+
+    def ahead(blocks):
+        for m in blocks:
+            span = pl.ds(pl.multiple_of(m * T, T), T)
+            for g in (early, middle):
+                pre[g, span, :] = project(span, g)
+
+    hops = [(0, 0), (0, 1), (1, 0), (1, 1)]
+    for dx, dy in hops[:3]:
+        m = features(dx, dy, 1)
+        landed(rows(x_all, m, T), x_r.at[m])
+    arrived(early, jnp.logical_and(jnp.logical_not(found0), outer))
+    arrived(middle, outer)
+    ahead([features(dx, dy, core) for dx, dy in hops[:3] for core in range(2)])
+    relay(1, 1, (partner,))
+    m = features(1, 1, 1)
+    landed(rows(x_all, m, T), x_r.at[m])
+    ahead([features(1, 1, core) for core in range(2)])
+    arrived(late, jnp.logical_or(found3, outer))
 
     group = pl.ds(pl.multiple_of(k * hb, hb), hb)
     rz, rr, rc = (recur[i : i + 1, group] for i in range(GATES))
     bz, br, bc = (bias[i : i + 1, group] for i in range(GATES))
-    for dx, dy in hops:
-        for core in range(2):
-            m = 2 * (2 * ((x + dx) % nx) + (c + core) % 2) + (y + dy) % 2
-            if core:
-                landed(rows(x_all, m, T), x_r.at[m])
-            span = pl.ds(pl.multiple_of(m * T, T), T)
-            pre = lax.dot_general(
-                x_all[span, :], w_all[...], (((1,), (1,)), ((), ())), preferred_element_type=F32
-            )
-            prior = prior_all[span, :]
-            gz = jax.nn.sigmoid(pre[:, :hb] + rz * prior + bz)
-            gr = jax.nn.sigmoid(pre[:, hb : 2 * hb] + rr * prior + br)
-            rp = gr * prior
-            gc = jnp.tanh(pre[:, 2 * hb :] + rc * rp + bc)
-            az = (gc - prior) * gz * (1.0 - gz)
-            ac = gz * (1.0 - gc * gc)
-            slope = rp * (1.0 - gr)
-            acr = ac * rc
-            co_z[span, :] = az
-            co_c[span, :] = ac
-            co_r[span, :] = acr * slope
-            rprior[span, :] = rp
-            jac[span, :] = same_all[span, :] * (1.0 - gz + az * rz + acr * (gr + slope * rr))
-
     for m in range(nh):
-        landed(up_in.at[m], v_r.at[m])
-        up[m * T : (m + 1) * T, :] = up_in[m].astype(F32)
+        span = slice(m * T, (m + 1) * T)
+        last = project(span, late)
+        pz, pr, pc = (jnp.where(late == i, last, pre[i, span, :]) for i in range(GATES))
+        prior = prior_all[span, :]
+        gz = jax.nn.sigmoid(pz + rz * prior + bz)
+        gr = jax.nn.sigmoid(pr + rr * prior + br)
+        rp = gr * prior
+        gc = jnp.tanh(pc + rc * rp + bc)
+        az = (gc - prior) * gz * (1.0 - gz)
+        ac = gz * (1.0 - gc * gc)
+        slope = rp * (1.0 - gr)
+        acr = ac * rc
+        co_z[span, :] = az
+        co_c[span, :] = ac
+        co_r[span, :] = acr * slope
+        rprior[span, :] = rp
+        jac[m * stride : m * stride + T, :] = same_all[span, :] * (
+            1.0 - gz + az * rz + acr * (gr + slope * rr)
+        )
+
+    landed(up_in, v_r)
+    for m in range(nh):
+        up[m * stride : m * stride + T, :] = up_in[m].astype(F32)
 
     def back(i, state):
         a, b = state
         t = T - 1 - i
-        f = jac[pl.ds(t, nh, stride=T), :]
-        b = b + up[pl.ds(t, nh, stride=T), :]
+        f = jac[pl.ds(t, nh, stride=stride), :]
+        b = b + up[pl.ds(t, nh, stride=stride), :]
         scan_a[t] = a
         scan_b[t] = b
         return f * a, f * b
@@ -363,7 +382,8 @@
         seg_out[0, o : o + 1, :] = a[first, :] * a[second, :]
         seg_out[1, o : o + 1, :] = b[first, :] + a[first, :] * b[second, :]
     for plane in range(nz - 1):
-        send_if(plane < z, seg_out, seg_in.at[z], c_s.at[plane], c_r.at[z], at(plane, k))
+        send_if(plane < z, seg_out, seg_in.at[z], c_s, c_r.at[z], at(plane, k))
+        unsent.append((z == plane + 1, seg_in.at[0 : plane + 1], c_s))
     carry[...] = jnp.zeros(carry.shape, F32)
     for plane in reversed(range(1, nz)):
 
@@ -381,7 +401,7 @@
     carried = jnp.concatenate(carry_rows, 0)
 
     def finish(t, _):
-        lam[pl.ds(t, nh, stride=T), :] = scan_b[t] + scan_a[t] * carried
+        lam[pl.ds(t, nh, stride=stride), :] = scan_b[t] + scan_a[t] * carried
         return 0
 
     lax.fori_loop(0, T, finish, 0, unroll=8)
@@ -390,7 +410,7 @@
     for m in range(nh):
         span = slice(m * T, (m + 1) * T)
         prior = prior_all[span, :]
-        adj = lam[span, :]
+        adj = lam[m * stride : m * stride + T, :]
         grad_z = adj * co_z[span, :]
         grad_r = adj * co_r[span, :]
         grad_c = adj * co_c[span, :]
@@ -404,7 +424,8 @@
     st_out[6:8, :] = jnp.zeros((2, hb), F32)
     st_z[z] = st_out[...]
     for plane in range(nz):
-        send_if(plane != z, st_out, st_z.at[z], t_s.at[plane], t_r.at[z], column(plane))
+        send_if(plane != z, st_out, st_z.at[z], t_s, t_r, column(plane))
+    unsent.append((True, st_z.at[0 : nz - 1], t_s))
 
     def quarter(col):
         return slice(col * cw, (col + 1) * cw)
@@ -426,13 +447,13 @@
         for col in range(nr):
             part = wg_out.at[g, :, quarter(col)]
             send_if(
-                inward, part, wg_end.at[g, :, quarter(col)], g_s.at[step * nr + col],
+                inward, part, wg_end.at[g, :, quarter(col)], g_s.at[step],
                 g_e.at[g * nr + col], column(high + half - 1),
             )
             send_if(
-                outward, part, wg_mid.at[0, :, quarter(col)], g_s.at[step * nr + col],
-                g_m.at[col], column(end),
+                outward, part, wg_mid.at[0, :, quarter(col)], g_s.at[step], g_m.at[col], column(end),
             )
+        unsent.append((plane != z, wg_out.at[step], g_s.at[step]))
 
     chips = [(x + 1, y + 1), (x + 1, y), (x, y + 1), (x, y)]
 
@@ -441,38 +462,38 @@
 
     for n in range(len(chips)):
         part_out[n] = jnp.dot(tokens(n, 1 - c), w_all[...], preferred_element_type=F32).astype(BF16)
-        send_if(True, part_out.at[n], part_in.at[n], d_s.at[n], d_r.at[n], partner)
+        send(part_out.at[n], part_in.at[n], d_s, d_r, partner)
     for n in range(len(chips)):
         part_keep[n] = jnp.dot(tokens(n, c), w_all[...], preferred_element_type=F32)
 
-    first = place(2 * z + (y + c) % 2, 2 * ((x + 1 - c) % nx) + c)
-    second = place(2 * z + (y + 1 - c) % 2, 2 * ((x + c) % nx) + c)
+    unsent.append((True, part_out, d_s))
+    unsent.append((True, fin_out, f_s))
 
     def both(n):
-        landed(part_in.at[n], d_r.at[n])
         return part_keep[n] + part_in[n].astype(F32)
 
+    landed(part_in, d_r)
     fin_out[0] = both(0).astype(BF16)
-    send_if(True, fin_out.at[0], fin_in.at[0], f_s.at[0], f_r.at[0], first)
+    send(fin_out.at[0], fin_in.at[0], f_s, f_r.at[0], nearest)
     fin_out[1] = both(1 + c).astype(BF16)
-    send_if(True, fin_out.at[1], fin_in.at[1], f_s.at[1], f_r.at[1], first)
+    send(fin_out.at[1], fin_in.at[1], f_s, f_r.at[1], nearest)
 
     scale = 1.0 / math.sqrt(ns * nr * T)
-    for plane in range(nz):
-        pl.when(plane != z)(functools.partial(landed, st_z.at[plane], t_r.at[plane]))
+    landed(st_z.at[0 : nz - 1], t_r)
     total = st_z[0]
     for plane in range(1, nz):
         total = total + st_z[plane]
     st_sum[...] = total * scale
     st_all[k] = st_sum[...]
     for j in range(nh):
-        send_if(j != k, st_sum, st_all.at[k], u_s.at[j], u_r.at[k], at(z, j))
+        send_if(j != k, st_sum, st_all.at[k], u_s, u_r, at(z, j))
+    unsent.append((True, st_all.at[0 : nh - 1], u_s))
 
     def turn():
         total = both(2 - c)
         landed(fin_in.at[0], f_r.at[0])
         fin_out[2] = (total + fin_in[0].astype(F32)).astype(BF16)
-        send_if(True, fin_out.at[2], fin_in.at[2], f_s.at[2], f_r.at[2], second)
+        send(fin_out.at[2], fin_in.at[2], f_s, f_r.at[2], across)
 
     for step in range(GATES):
         if step == 1:
@@ -491,7 +512,7 @@
             for slot, there in enumerate((jnp.logical_not(far), far)):
                 send_if(
                     jnp.logical_and(passed, there), wg_out.at[g, :, cols], wg_mid.at[slot, :, cols],
-                    g_s.at[step * nr + col], g_m.at[slot * nr + col], column(plane),
+                    g_s.at[step], g_m.at[slot * nr + col], column(plane),
                 )
 
     _, g, found = origin(0)
@@ -523,11 +544,13 @@
 
         send_if(
             jnp.logical_and(found, jnp.logical_not(here)), wg_out.at[g, :, cols], wg_in.at[i],
-            g_f.at[col], g_r.at[i], place(owner, col),
+            g_f, g_r.at[i], place(owner, col),
         )
-
+    unsent.append((jnp.logical_and(found, owner != s), wg_out.at[0], g_f))
+    unsent.append((jnp.logical_and(found, owner == s), wg_out.at[0, :, 0 : (nr - 1) * cw], g_f))
+
+    landed(st_all.at[0 : nh - 1], u_r)
     for j in range(nh):
-        pl.when(j != k)(functools.partial(landed, st_all.at[j], u_r.at[j]))
         out_p[:, j * hb : (j + 1) * hb] = st_all[j, :6, :]
 
     total = both(3)
@@ -573,11 +596,9 @@
         vm((GATES, H), F32),
         vm((GATES, H), F32),
         vm((T, H), BF16),
+        vm((nh, T + 16, hb), BF16),
+        vm((nh, T + 16, hb), BF16),
         vm((nh, T, hb), BF16),
-        vm((nh, T, hb), BF16),
-        vm((nh, T, hb), BF16),
-        vm((8, T), F32),
-        vm((nh, 8, T), F32),
         vm((8, H), F32),
         vm((8, H), F32),
         vm((nr, 8, hb), F32),
@@ -586,8 +607,9 @@
         vm((L + 8 * nh, hb), F32),
         vm((L + 8 * nh, hb), F32),
         vm((L, hb), F32),
-        vm((L, hb), F32),
-        vm((L, hb), F32),
+        vm((L + 8 * nh, hb), F32),
+        vm((GATES, L, hb), F32),
+        vm((L + 8 * nh, hb), F32),
         vm((L, hb), F32),
         vm((L, hb), F32),
         vm((L, hb), F32),
@@ -598,7 +620,7 @@
         vm((nh, hb), F32),
         vm((2, 8, hb), F32),
         vm((nz, 2, 8, hb), F32),
-        vm((L, hb), F32),
+        vm((L + 8 * nh, hb), F32),
         vm((L, GATES * hb), BF16),
         vm((nr, T, DI), BF16),
         vm((nr, T, DI), BF16),
@@ -618,8 +640,8 @@
     ]
     dma = pltpu.SemaphoreType.DMA
     counts = [
-        7, nr * nx, nr, nr, nh, GATES, nz * nr, GATES * nr, nh, nh, nh, nh, nh, nh, nh, nr, None, None,
-        nz, nz, nr, nr, 3, 3, GATES * nr, GATES * nr, 2 * nr, nr, GATES, nz, nz, nh, nh,
+        7, None, nh, GATES, nz - 1, GATES * nr, None, None, None, None, None, None, None, None, None, nz,
+        None, None, None, 3, GATES, GATES * nr, 2 * nr, None, GATES, None, None, None, None,
     ]
     sems = [dma if n is None else dma((n,)) for n in counts]
     whole = pl.BlockSpec(memory_space=pltpu.VMEM)
@@ -656,6 +678,7 @@
         and ns == 2 * nr
         and ns % 8 == 0
         and ns == 8
+        and L * 2 * nr == H * ns
         and H % (ns * 128) == 0
         and DI % (nr * 128) == 0
         and L % (ns * 128) == 0

time: 53.4 us -> 49.7 us (0.931)
  the two profiles are of different devices: /device:TPU:3 before, /device:TPU:1 now
where the time goes in v4:
time: 49.7 us; the launch traced here: 48.8 us
  Pallas kernels  48.2 us (97%)
  between operations  0.64 us (1%)
    pallas_call x1, Pallas kernels, by_hidden(): pl.pallas_call(functools.partial(kernel, ns, nr), out_shape=(pltpu.VMEM((...  47.3 us

profile of v4, /device:TPU:1, one launch (start us, length us, event | category | flops | bytes accessed | tf_op | source)
XLA Modules:
  0.0 48.8 jit_solution(12819981602477557548)
XLA Ops:
  0.6 47.3 %shard_map.94 = (bf16[128,1024]{1,0:T(8,128)(2,1)S(1)}, f32[384,256]{1,0:T(8,128)S(1)}, f32[6,1024]{1,0:T(8,128)S(1)}) custom-call(bf16[128,1024]{1,0:T(8,128)(2,1)} %bitcast.5, bf16[384,256]{1,0:T(8,128)(2,1)} %weight_hbm.1, f32[128,1024]{1,0:T(8,128)} %bitcast.4, s32[1,128]{1,0:T(1,128)} %ids_hbm.1, f32[3,1024]{1,0:T(4,128)} %recur_hbm.1, ...), custom_call_target="tpu_custom_call" | custom-call | tf_op jit(solution)/shard_map/pallas_call | solution.py:648
  47.9 0.9 %shard_map.95 = (bf16[128,1024]{1,0:T(8,128)(2,1)}, f32[384,256]{1,0:T(8,128)}, f32[6,1024]{1,0:T(8,128)}) custom-call(bf16[128,1024]{1,0:T(8,128)(2,1)S(1)} %get-tuple-element.9.in_a, f32[384,256]{1,0:T(8,128)S(1)} %get-tuple-element.10.in_b, f32[6,1024]{1,0:T(8,128)S(1)} %get-tuple-element.11.in_c), custom_call_target="tpu_custom_call" | custom-call | tf_op jit(solution)/shard_map/pallas_call | solution.py:663

commit v5 on v4

--- a/solution.py
+++ b/solution.py
@@ -96,10 +96,10 @@
     weight, states, ids, recur, bias, upstream,
     pay_src, pay, up_in, tail_src, tail_mid, tail_in, x_all, w_all, prev, ids_col, same_all, up,
     pre, jac, co_z, co_r, co_c, rprior, prior_all,
-    scan_a, scan_b, carry, seg_out, seg_in, lam, grads, part_out, part_in, part_keep, fin_out, fin_in,
+    scan_a, scan_b, carry, seg_out, seg_in, lam, grads, wg_via, part_out, part_in, part_keep, fin_out, fin_in,
     wg_own, wg_out, wg_end, wg_mid, wg_fin, wg_in, st_out, st_z, st_sum, st_all,
     l_s, x_s, x_r, w_s, w_f, w_r, p_s, p_r, v_s, v_r, e_s, e_r, n_s, n_r, c_s, c_r,
-    d_s, d_r, f_s, f_r, g_s, g_e, g_m, g_f, g_r, t_s, t_r, u_s, u_r,
+    d_s, d_r, f_s, f_r, g_s, g_e, g_m, g_f, g_r, t_s, t_r, u_s, u_r, h_s, h_r,
 ):
     T, DI = feats_hbm.shape
     H = states.shape[1]
@@ -261,11 +261,6 @@
     relay(c, 1 - c, (nearest, partner))
     spread(1, range(nr // 2, nr))
     relay(1 - c, c, (partner,))
-    loaded(4)
-    for j in range(nh):
-        part = upstream.at[:, j * hb : (j + 1) * hb]
-        send_or_local(part, up_in.at[q], v_s, v_r, at(z, j), k == j)
-    unsent.append((True, up_in.at[0 : nh - 1], v_s))
     spread(2, range(nr))
 
     stride = T + 8
@@ -332,6 +327,11 @@
     arrived(early, jnp.logical_and(jnp.logical_not(found0), outer))
     arrived(middle, outer)
     ahead([features(dx, dy, core) for dx, dy in hops[:3] for core in range(2)])
+    loaded(4)
+    for j in range(nh):
+        part = upstream.at[:, j * hb : (j + 1) * hb]
+        send_or_local(part, up_in.at[q], v_s, v_r, at(z, j), k == j)
+    unsent.append((True, up_in.at[0 : nh - 1], v_s))
     relay(1, 1, (partner,))
     m = features(1, 1, 1)
     landed(rows(x_all, m, T), x_r.at[m])
@@ -371,8 +371,8 @@
         t = T - 1 - i
         f = jac[pl.ds(t, nh, stride=stride), :]
         b = b + up[pl.ds(t, nh, stride=stride), :]
-        scan_a[t] = a
-        scan_b[t] = b
+        scan_a[pl.ds(t, nh, stride=stride), :] = a
+        scan_b[pl.ds(t, nh, stride=stride), :] = b
         return f * a, f * b
 
     a, b = lax.fori_loop(0, T, back, (jnp.ones((nh, hb), F32), jnp.zeros((nh, hb), F32)), unroll=8)
@@ -400,32 +400,13 @@
         carry_rows += [b[second, :] + a[second, :] * later, later]
     carried = jnp.concatenate(carry_rows, 0)
 
-    def finish(t, _):
-        lam[pl.ds(t, nh, stride=stride), :] = scan_b[t] + scan_a[t] * carried
-        return 0
-
-    lax.fori_loop(0, T, finish, 0, unroll=8)
-
-    sums = [jnp.zeros((1, hb), F32) for _ in range(6)]
     for m in range(nh):
         span = slice(m * T, (m + 1) * T)
-        prior = prior_all[span, :]
-        adj = lam[m * stride : m * stride + T, :]
-        grad_z = adj * co_z[span, :]
-        grad_r = adj * co_r[span, :]
-        grad_c = adj * co_c[span, :]
-        grads[span, :hb] = grad_z.astype(BF16)
-        grads[span, hb : 2 * hb] = grad_r.astype(BF16)
-        grads[span, 2 * hb :] = grad_c.astype(BF16)
-        terms = (grad_z, grad_r, grad_c, grad_z * prior, grad_r * prior, grad_c * rprior[span, :])
-        sums = [total + jnp.sum(term, 0, keepdims=True) for total, term in zip(sums, terms)]
-    for i in range(6):
-        st_out[i : i + 1, :] = sums[i]
-    st_out[6:8, :] = jnp.zeros((2, hb), F32)
-    st_z[z] = st_out[...]
-    for plane in range(nz):
-        send_if(plane != z, st_out, st_z.at[z], t_s, t_r, column(plane))
-    unsent.append((True, st_z.at[0 : nz - 1], t_s))
+        padded = slice(m * stride, m * stride + T)
+        adj = scan_b[padded, :] + scan_a[padded, :] * carried[m : m + 1, :]
+        lam[span, :] = adj
+        for g, slope in enumerate((co_z, co_r, co_c)):
+            grads[span, g * hb : (g + 1) * hb] = (adj * slope[span, :]).astype(BF16)
 
     def quarter(col):
         return slice(col * cw, (col + 1) * cw)
@@ -434,8 +415,45 @@
         g = high * step + (1 - high) * (GATES - 1 - step)
         return g, (nh * g + k) // per
 
-    for step in range(GATES):
-        g, plane = gate_of(step)
+    def short(hidden):
+        g = (per * z - hidden + nh - 1) // nh
+        have = jnp.logical_and(g < GATES, nh * g + hidden < per * (z + 1))
+        return jnp.logical_and(outer, jnp.logical_not(have))
+
+    lacks, helps = short(k), short(2 * nx * c + 2 * ((x + 1) % nx) + y)
+    beside = place(s, 2 * ((x + 1) % nx) + c)
+    hub = high + half - 1
+    halves = slice(nr // 2 * cw, DI)
+
+    near = inner.astype(jnp.int32)
+    turns = (
+        (GATES - 1) * (high * near + (1 - high) * (1 - near)),
+        (GATES - 1) * (1 - high) * near + 1 - near,
+        near + (GATES - 1) * high * (1 - near),
+    )
+
+    def statistics():
+        sums = [jnp.zeros((1, hb), F32) for _ in range(6)]
+        for m in range(nh):
+            span = slice(m * T, (m + 1) * T)
+            prior = prior_all[span, :]
+            adj = lam[span, :]
+            grad_z = adj * co_z[span, :]
+            grad_r = adj * co_r[span, :]
+            grad_c = adj * co_c[span, :]
+            terms = (grad_z, grad_r, grad_c, grad_z * prior, grad_r * prior, grad_c * rprior[span, :])
+            sums = [total + jnp.sum(term, 0, keepdims=True) for total, term in zip(sums, terms)]
+        for i in range(6):
+            st_out[i : i + 1, :] = sums[i]
+        st_out[6:8, :] = jnp.zeros((2, hb), F32)
+        st_z[z] = st_out[...]
+        for plane in range(nz):
+            send_if(plane != z, st_out, st_z.at[z], t_s, t_r, column(plane))
+        unsent.append((True, st_z.at[0 : nz - 1], t_s))
+
+    def weigh(step):
+        g = turns[step]
+        plane = (nh * g + k) // per
         block = lax.dot_general(
             grads[:, pl.ds(pl.multiple_of(g * hb, hb), hb)], x_all[...], (((0,), (0,)), ((), ())),
             preferred_element_type=F32,
@@ -443,51 +461,89 @@
         wg_own[g] = block
         wg_out[g] = block.astype(BF16)
         outward = jnp.logical_and(inner, plane == end)
-        inward = jnp.logical_and(jnp.logical_not(inner), plane != z)
+        inward = jnp.logical_and(outer, plane != z)
         for col in range(nr):
+            if step == 0 and col == nr // 2:
+                statistics()
             part = wg_out.at[g, :, quarter(col)]
             send_if(
-                inward, part, wg_end.at[g, :, quarter(col)], g_s.at[step],
-                g_e.at[g * nr + col], column(high + half - 1),
+                jnp.logical_and(inward, plane != hub), part, wg_end.at[g, :, quarter(col)], g_s.at[g],
+                g_e.at[g * nr + col], column(hub),
             )
             send_if(
-                outward, part, wg_mid.at[0, :, quarter(col)], g_s.at[step], g_m.at[col], column(end),
+                outward, part, wg_mid.at[0, :, quarter(col)], g_s.at[g], g_m.at[col], column(end),
             )
-        unsent.append((plane != z, wg_out.at[step], g_s.at[step]))
+        if step == GATES - 1:
+            send_if(lacks, wg_out.at[g, :, halves], wg_via, g_s.at[g], h_r, beside)
+        unsent.append((plane != z, wg_out.at[g], g_s.at[g]))
+
+    def nearby(step):
+        g, plane = gate_of(step)
+        for col in range(nr):
+            go = jnp.logical_and(outer, plane == hub)
+            if step == GATES - 1 and col >= nr // 2:
+                go = jnp.logical_and(go, jnp.logical_not(lacks))
+            send_if(
+                go, wg_out.at[g, :, quarter(col)], wg_end.at[g, :, quarter(col)], g_s.at[g],
+                g_e.at[g * nr + col], column(hub),
+            )
+
+    def assist():
+        g, _ = gate_of(GATES - 1)
+        pl.when(helps)(functools.partial(landed, wg_via, h_r))
+        for col in range(nr // 2, nr):
+            part = wg_via.at[:, (col - nr // 2) * cw : (col - nr // 2 + 1) * cw]
+            where = place(2 * hub + y, 2 * ((x + 1) % nx) + c)
+            send_if(helps, part, wg_end.at[g, :, quarter(col)], h_s, g_e.at[g * nr + col], where)
+        unsent.append((helps, wg_via, h_s))
 
     chips = [(x + 1, y + 1), (x + 1, y), (x, y + 1), (x, y)]
+    lot = (0, 1, 1, 2)
 
     def tokens(n, core):
         return rows(grads, 2 * (2 * (chips[n][0] % nx) + core) + chips[n][1] % 2, T)[...]
 
-    for n in range(len(chips)):
+    def give(n):
         part_out[n] = jnp.dot(tokens(n, 1 - c), w_all[...], preferred_element_type=F32).astype(BF16)
-        send(part_out.at[n], part_in.at[n], d_s, d_r, partner)
-    for n in range(len(chips)):
+        send(part_out.at[n], part_in.at[n], d_s, d_r.at[lot[n]], partner)
+
+    def keep(n):
         part_keep[n] = jnp.dot(tokens(n, c), w_all[...], preferred_element_type=F32)
 
+    def both(n):
+        return part_keep[n] + part_in[n].astype(F32)
+
+    weigh(0)
+    give(0)
+    keep(0)
+    weigh(1)
+    give(1)
+    give(2)
+    landed(part_in.at[0], d_r.at[0])
+    fin_out[0] = both(0).astype(BF16)
+    send(fin_out.at[0], fin_in.at[0], f_s, f_r.at[0], nearest)
+    weigh(2)
+    keep(1)
+    keep(2)
+    landed(part_in.at[1:3], d_r.at[1])
+    fin_out[1] = both(1 + c).astype(BF16)
+    send(fin_out.at[1], fin_in.at[1], f_s, f_r.at[1], nearest)
+    give(3)
+    keep(3)
     unsent.append((True, part_out, d_s))
     unsent.append((True, fin_out, f_s))
 
-    def both(n):
-        return part_keep[n] + part_in[n].astype(F32)
-
-    landed(part_in, d_r)
-    fin_out[0] = both(0).astype(BF16)
-    send(fin_out.at[0], fin_in.at[0], f_s, f_r.at[0], nearest)
-    fin_out[1] = both(1 + c).astype(BF16)
-    send(fin_out.at[1], fin_in.at[1], f_s, f_r.at[1], nearest)
-
     scale = 1.0 / math.sqrt(ns * nr * T)
-    landed(st_z.at[0 : nz - 1], t_r)
-    total = st_z[0]
-    for plane in range(1, nz):
-        total = total + st_z[plane]
-    st_sum[...] = total * scale
-    st_all[k] = st_sum[...]
-    for j in range(nh):
-        send_if(j != k, st_sum, st_all.at[k], u_s, u_r, at(z, j))
-    unsent.append((True, st_all.at[0 : nh - 1], u_s))
+    def gather_stats():
+        landed(st_z.at[0 : nz - 1], t_r)
+        total = st_z[0]
+        for plane in range(1, nz):
+            total = total + st_z[plane]
+        st_sum[...] = total * scale
+        st_all[k] = st_sum[...]
+        for j in range(nh):
+            send_if(j != k, st_sum, st_all.at[k], u_s, u_r, at(z, j))
+        unsent.append((True, st_all.at[0 : nh - 1], u_s))
 
     def turn():
         total = both(2 - c)
@@ -498,6 +554,9 @@
     for step in range(GATES):
         if step == 1:
             turn()
+            for other in range(GATES):
+                nearby(other)
+            assist()
         g, plane = gate_of(step)
         passed = jnp.logical_and(inner, jnp.logical_and(plane != z, plane != end))
         far = (plane // half != high) & ((plane == 0) | (plane == nz - 1))
@@ -512,9 +571,10 @@
             for slot, there in enumerate((jnp.logical_not(far), far)):
                 send_if(
                     jnp.logical_and(passed, there), wg_out.at[g, :, cols], wg_mid.at[slot, :, cols],
-                    g_s.at[step], g_m.at[slot * nr + col], column(plane),
+                    g_s.at[g], g_m.at[slot * nr + col], column(plane),
                 )
 
+    gather_stats()
     _, g, found = origin(0)
     b = nh * g + k
     owner, i = b // GATES, b % GATES
@@ -553,6 +613,7 @@
     for j in range(nh):
         out_p[:, j * hb : (j + 1) * hb] = st_all[j, :6, :]
 
+    landed(part_in.at[3], d_r.at[2])
     total = both(3)
     for n in (1, 2):
         landed(fin_in.at[n], f_r.at[n])
@@ -615,13 +676,14 @@
         vm((L, hb), F32),
         vm((L, hb), F32),
         vm((L, hb), F32),
-        vm((T, nh, hb), F32),
-        vm((T, nh, hb), F32),
+        vm((L + 8 * nh, hb), F32),
+        vm((L + 8 * nh, hb), F32),
         vm((nh, hb), F32),
         vm((2, 8, hb), F32),
         vm((nz, 2, 8, hb), F32),
-        vm((L + 8 * nh, hb), F32),
+        vm((L, hb), F32),
         vm((L, GATES * hb), BF16),
+        vm((hb, DI // 2), BF16),
         vm((nr, T, DI), BF16),
         vm((nr, T, DI), BF16),
         vm((nr, T, DI), F32),
@@ -641,7 +703,7 @@
     dma = pltpu.SemaphoreType.DMA
     counts = [
         7, None, nh, GATES, nz - 1, GATES * nr, None, None, None, None, None, None, None, None, None, nz,
-        None, None, None, 3, GATES, GATES * nr, 2 * nr, None, GATES, None, None, None, None,
+        None, 3, None, 3, GATES, GATES * nr, 2 * nr, None, GATES, None, None, None, None, None, None,
     ]
     sems = [dma if n is None else dma((n,)) for n in counts]
     whole = pl.BlockSpec(memory_space=pltpu.VMEM)

time: 49.7 us -> 48.5 us (0.976); the launches traced: 48.8 us -> 48.4 us
  Pallas kernels: 48.2 us -> 47.7 us
where the time goes in v5:
time: 48.5 us; the launch traced here: 48.4 us
  Pallas kernels  47.7 us (98%)
  between operations  0.64 us (1%)
    pallas_call x1, Pallas kernels, by_hidden(): pl.pallas_call(functools.partial(kernel, ns, nr), out_shape=(pltpu.VMEM((...  46.9 us

profile of v5, /device:TPU:1, one launch (start us, length us, event | category | flops | bytes accessed | tf_op | source)
XLA Modules:
  0.0 48.4 jit_solution(2829931754605967679)
XLA Ops:
  0.6 46.9 %shard_map.94 = (bf16[128,1024]{1,0:T(8,128)(2,1)S(1)}, f32[384,256]{1,0:T(8,128)S(1)}, f32[6,1024]{1,0:T(8,128)S(1)}) custom-call(bf16[128,1024]{1,0:T(8,128)(2,1)} %bitcast.5, bf16[384,256]{1,0:T(8,128)(2,1)} %weight_hbm.1, f32[128,1024]{1,0:T(8,128)} %bitcast.4, s32[1,128]{1,0:T(1,128)} %ids_hbm.1, f32[3,1024]{1,0:T(4,128)} %recur_hbm.1, ...), custom_call_target="tpu_custom_call" | custom-call | tf_op jit(solution)/shard_map/pallas_call | solution.py:710
  47.5 0.9 %shard_map.95 = (bf16[128,1024]{1,0:T(8,128)(2,1)}, f32[384,256]{1,0:T(8,128)}, f32[6,1024]{1,0:T(8,128)}) custom-call(bf16[128,1024]{1,0:T(8,128)(2,1)S(1)} %get-tuple-element.9.in_a, f32[384,256]{1,0:T(8,128)S(1)} %get-tuple-element.10.in_b, f32[6,1024]{1,0:T(8,128)S(1)} %get-tuple-element.11.in_c), custom_call_target="tpu_custom_call" | custom-call | tf_op jit(solution)/shard_map/pallas_call | solution.py:725

commit v6 on v5

--- a/solution.py
+++ b/solution.py
@@ -97,7 +97,7 @@
     pay_src, pay, up_in, tail_src, tail_mid, tail_in, x_all, w_all, prev, ids_col, same_all, up,
     pre, jac, co_z, co_r, co_c, rprior, prior_all,
     scan_a, scan_b, carry, seg_out, seg_in, lam, grads, wg_via, part_out, part_in, part_keep, fin_out, fin_in,
-    wg_own, wg_out, wg_end, wg_mid, wg_fin, wg_in, st_out, st_z, st_sum, st_all,
+    wg_own, wg_out, wg_end, wg_mid, wg_in, st_out, st_z, st_sum, st_all,
     l_s, x_s, x_r, w_s, w_f, w_r, p_s, p_r, v_s, v_r, e_s, e_r, n_s, n_r, c_s, c_r,
     d_s, d_r, f_s, f_r, g_s, g_e, g_m, g_f, g_r, t_s, t_r, u_s, u_r, h_s, h_r,
 ):
@@ -261,6 +261,20 @@
     relay(c, 1 - c, (nearest, partner))
     spread(1, range(nr // 2, nr))
     relay(1 - c, c, (partner,))
+    loaded(4)
+
+    def send_upstream(early):
+        for j in range(nh):
+            part = upstream.at[:, j * hb : (j + 1) * hb]
+            over_x, over_y = j // 2 % nx != x, j % 2 != y
+            other_link = jnp.where(c == 0, jnp.logical_and(over_y, jnp.logical_not(over_x)), over_x)
+            now = jnp.logical_not(other_link) if early else other_link
+            send_if(jnp.logical_and(now, j != k), part, up_in.at[q], v_s, v_r, at(z, j))
+            if early:
+                pl.when(j == k)(functools.partial(local, part, up_in.at[q], v_r))
+
+    unsent.append((True, up_in.at[0 : nh - 1], v_s))
+    send_upstream(True)
     spread(2, range(nr))
 
     stride = T + 8
@@ -327,15 +341,12 @@
     arrived(early, jnp.logical_and(jnp.logical_not(found0), outer))
     arrived(middle, outer)
     ahead([features(dx, dy, core) for dx, dy in hops[:3] for core in range(2)])
-    loaded(4)
-    for j in range(nh):
-        part = upstream.at[:, j * hb : (j + 1) * hb]
-        send_or_local(part, up_in.at[q], v_s, v_r, at(z, j), k == j)
-    unsent.append((True, up_in.at[0 : nh - 1], v_s))
+    send_upstream(False)
     relay(1, 1, (partner,))
+    ahead([features(1, 1, 0)])
     m = features(1, 1, 1)
     landed(rows(x_all, m, T), x_r.at[m])
-    ahead([features(1, 1, core) for core in range(2)])
+    ahead([m])
     arrived(late, jnp.logical_or(found3, outer))
 
     group = pl.ds(pl.multiple_of(k * hb, hb), hb)
@@ -420,7 +431,8 @@
         have = jnp.logical_and(g < GATES, nh * g + hidden < per * (z + 1))
         return jnp.logical_and(outer, jnp.logical_not(have))
 
-    lacks, helps = short(k), short(2 * nx * c + 2 * ((x + 1) % nx) + y)
+    other = 2 * nx * c + 2 * ((x + 1) % nx) + y
+    lacks, helps = short(k), short(other)
     beside = place(s, 2 * ((x + 1) % nx) + c)
     hub = high + half - 1
     halves = slice(nr // 2 * cw, DI)
@@ -454,17 +466,24 @@
     def weigh(step):
         g = turns[step]
         plane = (nh * g + k) // per
-        block = lax.dot_general(
-            grads[:, pl.ds(pl.multiple_of(g * hb, hb), hb)], x_all[...], (((0,), (0,)), ((), ())),
-            preferred_element_type=F32,
-        )
-        wg_own[g] = block
-        wg_out[g] = block.astype(BF16)
+        spans = (slice(0, DI // 2), slice(DI // 2, DI)) if step == 0 else (slice(0, DI),)
+
+        def product(span):
+            block = lax.dot_general(
+                grads[:, pl.ds(pl.multiple_of(g * hb, hb), hb)], x_all[:, span], (((0,), (0,)), ((), ())),
+                preferred_element_type=F32,
+            )
+            wg_own[g, :, span] = block
+            wg_out[g, :, span] = block.astype(BF16)
+
+        product(spans[0])
         outward = jnp.logical_and(inner, plane == end)
         inward = jnp.logical_and(outer, plane != z)
         for col in range(nr):
-            if step == 0 and col == nr // 2:
+            if step == 0 and col == 1:
+                give(0)
                 statistics()
+                product(spans[1])
             part = wg_out.at[g, :, quarter(col)]
             send_if(
                 jnp.logical_and(inward, plane != hub), part, wg_end.at[g, :, quarter(col)], g_s.at[g],
@@ -513,27 +532,9 @@
     def both(n):
         return part_keep[n] + part_in[n].astype(F32)
 
-    weigh(0)
-    give(0)
-    keep(0)
-    weigh(1)
-    give(1)
-    give(2)
-    landed(part_in.at[0], d_r.at[0])
-    fin_out[0] = both(0).astype(BF16)
-    send(fin_out.at[0], fin_in.at[0], f_s, f_r.at[0], nearest)
-    weigh(2)
-    keep(1)
-    keep(2)
-    landed(part_in.at[1:3], d_r.at[1])
-    fin_out[1] = both(1 + c).astype(BF16)
-    send(fin_out.at[1], fin_in.at[1], f_s, f_r.at[1], nearest)
-    give(3)
-    keep(3)
-    unsent.append((True, part_out, d_s))
-    unsent.append((True, fin_out, f_s))
-
+    parts = [slice(n * T // 2, (n + 1) * T // 2) for n in range(2)]
     scale = 1.0 / math.sqrt(ns * nr * T)
+
     def gather_stats():
         landed(st_z.at[0 : nz - 1], t_r)
         total = st_z[0]
@@ -545,22 +546,18 @@
             send_if(j != k, st_sum, st_all.at[k], u_s, u_r, at(z, j))
         unsent.append((True, st_all.at[0 : nh - 1], u_s))
 
-    def turn():
-        total = both(2 - c)
-        landed(fin_in.at[0], f_r.at[0])
-        fin_out[2] = (total + fin_in[0].astype(F32)).astype(BF16)
-        send(fin_out.at[2], fin_in.at[2], f_s, f_r.at[2], across)
-
-    for step in range(GATES):
-        if step == 1:
-            turn()
-            for other in range(GATES):
-                nearby(other)
-            assist()
+    def turn(n):
+        part = parts[n]
+        landed(fin_in.at[0, part], f_r.at[n])
+        total = part_keep[2 - c, part] + part_in[2 - c, part].astype(F32) + fin_in[0, part].astype(F32)
+        fin_out[2, part] = total.astype(BF16)
+        send(fin_out.at[2, part], fin_in.at[2, part], f_s, f_r.at[3 + n], across)
+
+    def hand_on(step, numbers):
         g, plane = gate_of(step)
         passed = jnp.logical_and(inner, jnp.logical_and(plane != z, plane != end))
         far = (plane // half != high) & ((plane == 0) | (plane == nz - 1))
-        for col in range(nr):
+        for col in numbers:
             cols = quarter(col)
 
             @pl.when(passed)
@@ -574,7 +571,38 @@
                     g_s.at[g], g_m.at[slot * nr + col], column(plane),
                 )
 
+    weigh(0)
+    keep(0)
+    weigh(1)
+    landed(part_in.at[0], d_r.at[0])
+    fin_out[0] = both(0).astype(BF16)
+    for n, part in enumerate(parts):
+        send(fin_out.at[0, part], fin_in.at[0, part], f_s, f_r.at[n], nearest)
+    give(1)
+    give(2)
+    weigh(2)
+    hand_on(0, (0,))
+    keep(1)
+    keep(2)
+    landed(part_in.at[1:3], d_r.at[1])
+    fin_out[1] = both(1 + c).astype(BF16)
+    send(fin_out.at[1], fin_in.at[1], f_s, f_r.at[2], nearest)
+    hand_on(0, (1,))
+    give(3)
+    keep(3)
+    hand_on(0, (2,))
+    turn(0)
+    hand_on(0, (3,))
+    for n in range(GATES):
+        nearby(n)
     gather_stats()
+    turn(1)
+    assist()
+    for step in range(1, GATES):
+        hand_on(step, range(nr))
+    unsent.append((True, part_out, d_s))
+    unsent.append((True, fin_out, f_s))
+
     _, g, found = origin(0)
     b = nh * g + k
     owner, i = b // GATES, b % GATES
@@ -584,17 +612,21 @@
         @pl.when(found)
         def _():
             landed(wg_mid.at[0, :, cols], g_m.at[col])
-            wg_fin[:, cols] = wg_own[g, :, cols] + wg_mid[0, :, cols].astype(F32)
+            wg_own[g, :, cols] = wg_own[g, :, cols] + wg_mid[0, :, cols].astype(F32)
 
         @pl.when(jnp.logical_and(found, inner))
         def _():
             landed(wg_end.at[g, :, cols], g_e.at[g * nr + col])
-            wg_out[g, :, cols] = (wg_fin[:, cols] + wg_end[g, :, cols].astype(F32)).astype(BF16)
-
-        @pl.when(jnp.logical_and(found, jnp.logical_not(inner)))
+            wg_own[g, :, cols] = wg_own[g, :, cols] + wg_end[g, :, cols].astype(F32)
+
+        @pl.when(jnp.logical_and(found, outer))
         def _():
             landed(wg_mid.at[1, :, cols], g_m.at[nr + col])
-            wg_out[g, :, cols] = (wg_fin[:, cols] + wg_mid[1, :, cols].astype(F32)).astype(BF16)
+            wg_own[g, :, cols] = wg_own[g, :, cols] + wg_mid[1, :, cols].astype(F32)
+
+        @pl.when(found)
+        def _():
+            wg_out[g, :, cols] = wg_own[g, :, cols].astype(BF16)
 
         here = jnp.logical_and(owner == s, r == col)
 
@@ -615,14 +647,16 @@
 
     landed(part_in.at[3], d_r.at[2])
     total = both(3)
-    for n in (1, 2):
-        landed(fin_in.at[n], f_r.at[n])
-        total = total + fin_in[n].astype(F32)
+    landed(fin_in.at[1], f_r.at[2])
+    for n, part in enumerate(parts):
+        landed(fin_in.at[2, part], f_r.at[3 + n])
+    total = total + fin_in[1].astype(F32) + fin_in[2].astype(F32)
     out_in[...] = total.astype(BF16)
 
     for i in range(GATES):
         landed(wg_in.at[i], g_r.at[i])
-        out_w[i * hb : (i + 1) * hb, :] = wg_in[i].astype(F32) * scale
+        block = slice(i * hb, (i + 1) * hb)
+        out_w[block, :] = wg_in[i].astype(F32) * scale
 
     for sent, src, sem in unsent:
         if sent is True:
@@ -693,7 +727,6 @@
         vm((GATES, hb, DI), BF16),
         vm((GATES, hb, DI), BF16),
         vm((2, hb, DI), BF16),
-        vm((hb, DI), F32),
         vm((GATES, hb, cw), BF16),
         vm((8, hb), F32),
         vm((nz, 8, hb), F32),
@@ -703,7 +736,7 @@
     dma = pltpu.SemaphoreType.DMA
     counts = [
         7, None, nh, GATES, nz - 1, GATES * nr, None, None, None, None, None, None, None, None, None, nz,
-        None, 3, None, 3, GATES, GATES * nr, 2 * nr, None, GATES, None, None, None, None, None, None,
+        None, 3, None, 5, GATES, GATES * nr, 2 * nr, None, GATES, None, None, None, None, None, None,
     ]
     sems = [dma if n is None else dma((n,)) for n in counts]
     whole = pl.BlockSpec(memory_space=pltpu.VMEM)

time: 48.5 us -> 48 us (0.990); the launches traced: 48.4 us -> 47.3 us
  Pallas kernels: 47.7 us -> 46.7 us
    pallas_call x1, Pallas kernels: 46.9 us -> 45.8 us  [by_hidden(): pl.pallas_call(functools.partial(kernel, ns, nr), out_shape=(pltpu.VMEM((...]
where the time goes in v6:
time: 48 us; the launch traced here: 47.3 us
  Pallas kernels  46.7 us (97%)
  between operations  0.64 us (1%)
    pallas_call x1, Pallas kernels, by_hidden(): pl.pallas_call(functools.partial(kernel, ns, nr), out_shape=(pltpu.VMEM((...  45.8 us

profile of v6, /device:TPU:1, one launch (start us, length us, event | category | flops | bytes accessed | tf_op | source)
XLA Modules:
  0.0 47.3 jit_solution(4322676415282996058)
XLA Ops:
  0.6 45.8 %shard_map.94 = (bf16[128,1024]{1,0:T(8,128)(2,1)S(1)}, f32[384,256]{1,0:T(8,128)S(1)}, f32[6,1024]{1,0:T(8,128)S(1)}) custom-call(bf16[128,1024]{1,0:T(8,128)(2,1)} %bitcast.5, bf16[384,256]{1,0:T(8,128)(2,1)} %weight_hbm.1, f32[128,1024]{1,0:T(8,128)} %bitcast.4, s32[1,128]{1,0:T(1,128)} %ids_hbm.1, f32[3,1024]{1,0:T(4,128)} %recur_hbm.1, ...), custom_call_target="tpu_custom_call" | custom-call | tf_op jit(solution)/shard_map/pallas_call | solution.py:743
  46.4 0.9 %shard_map.95 = (bf16[128,1024]{1,0:T(8,128)(2,1)}, f32[384,256]{1,0:T(8,128)}, f32[6,1024]{1,0:T(8,128)}) custom-call(bf16[128,1024]{1,0:T(8,128)(2,1)S(1)} %get-tuple-element.9.in_a, f32[384,256]{1,0:T(8,128)S(1)} %get-tuple-element.10.in_b, f32[6,1024]{1,0:T(8,128)S(1)} %get-tuple-element.11.in_c), custom_call_target="tpu_custom_call" | custom-call | tf_op jit(solution)/shard_map/pallas_call | solution.py:758

commit v7 on v6

--- a/solution.py
+++ b/solution.py
@@ -343,35 +343,52 @@
     ahead([features(dx, dy, core) for dx, dy in hops[:3] for core in range(2)])
     send_upstream(False)
     relay(1, 1, (partner,))
-    ahead([features(1, 1, 0)])
-    m = features(1, 1, 1)
-    landed(rows(x_all, m, T), x_r.at[m])
-    ahead([m])
-    arrived(late, jnp.logical_or(found3, outer))
-
     group = pl.ds(pl.multiple_of(k * hb, hb), hb)
     rz, rr, rc = (recur[i : i + 1, group] for i in range(GATES))
     bz, br, bc = (bias[i : i + 1, group] for i in range(GATES))
-    for m in range(nh):
-        span = slice(m * T, (m + 1) * T)
-        last = project(span, late)
-        pz, pr, pc = (jnp.where(late == i, last, pre[i, span, :]) for i in range(GATES))
-        prior = prior_all[span, :]
-        gz = jax.nn.sigmoid(pz + rz * prior + bz)
-        gr = jax.nn.sigmoid(pr + rr * prior + br)
-        rp = gr * prior
-        gc = jnp.tanh(pc + rc * rp + bc)
-        az = (gc - prior) * gz * (1.0 - gz)
-        ac = gz * (1.0 - gc * gc)
-        slope = rp * (1.0 - gr)
-        acr = ac * rc
-        co_z[span, :] = az
-        co_c[span, :] = ac
-        co_r[span, :] = acr * slope
-        rprior[span, :] = rp
-        jac[m * stride : m * stride + T, :] = same_all[span, :] * (
-            1.0 - gz + az * rz + acr * (gr + slope * rr)
-        )
+
+    def gates(blocks):
+        for m in blocks:
+            whole = isinstance(m, int)
+            span = slice(m * T, (m + 1) * T) if whole else pl.ds(pl.multiple_of(m * T, T), T)
+            wide = slice(m * stride, m * stride + T) if whole else pl.ds(pl.multiple_of(m * stride, 8), T)
+            last = project(span, late)
+            pz, pr, pc = (jnp.where(late == i, last, pre[i, span, :]) for i in range(GATES))
+            prior = prior_all[span, :]
+            gz = jax.nn.sigmoid(pz + rz * prior + bz)
+            gr = jax.nn.sigmoid(pr + rr * prior + br)
+            rp = gr * prior
+            gc = jnp.tanh(pc + rc * rp + bc)
+            az = (gc - prior) * gz * (1.0 - gz)
+            ac = gz * (1.0 - gc * gc)
+            slope = rp * (1.0 - gr)
+            acr = ac * rc
+            co_z[span, :] = az
+            co_c[span, :] = ac
+            co_r[span, :] = acr * slope
+            rprior[span, :] = rp
+            jac[wide, :] = same_all[span, :] * (1.0 - gz + az * rz + acr * (gr + slope * rr))
+
+    def rest():
+        m = features(1, 1, 1)
+        landed(rows(x_all, m, T), x_r.at[m])
+        ahead([m])
+
+    ahead([features(1, 1, 0)])
+    missing = jnp.logical_or(found3, outer)
+
+    @pl.when(c == 1)
+    def _():
+        arrived(late, missing)
+        gates([features(dx, dy, core) for dx, dy in hops[:3] for core in range(2)])
+        rest()
+        gates([features(1, 1, core) for core in range(2)])
+
+    @pl.when(c == 0)
+    def _():
+        rest()
+        arrived(late, missing)
+        gates(range(nh))
 
     landed(up_in, v_r)
     for m in range(nh):
@@ -420,7 +437,12 @@
             grads[span, g * hb : (g + 1) * hb] = (adj * slope[span, :]).astype(BF16)
 
     def quarter(col):
-        return slice(col * cw, (col + 1) * cw)
+        return pl.ds(pl.multiple_of(col * cw, cw), cw)
+
+    away = [2 * ((x + 1 + n // 2) % nx) + n % 2 for n in range(nr)]
+
+    def side(n):
+        return pl.ds(pl.multiple_of(2 * ((x + n) % nx) * cw, 2 * cw), 2 * cw)
 
     def gate_of(step):
         g = high * step + (1 - high) * (GATES - 1 - step)
@@ -435,7 +457,6 @@
     lacks, helps = short(k), short(other)
     beside = place(s, 2 * ((x + 1) % nx) + c)
     hub = high + half - 1
-    halves = slice(nr // 2 * cw, DI)
 
     near = inner.astype(jnp.int32)
     turns = (
@@ -466,7 +487,7 @@
     def weigh(step):
         g = turns[step]
         plane = (nh * g + k) // per
-        spans = (slice(0, DI // 2), slice(DI // 2, DI)) if step == 0 else (slice(0, DI),)
+        spans = (side(1), side(0)) if step == 0 else (slice(0, DI),)
 
         def product(span):
             block = lax.dot_general(
@@ -479,8 +500,8 @@
         product(spans[0])
         outward = jnp.logical_and(inner, plane == end)
         inward = jnp.logical_and(outer, plane != z)
-        for col in range(nr):
-            if step == 0 and col == 1:
+        for n, col in enumerate(away):
+            if step == 0 and n == 1:
                 give(0)
                 statistics()
                 product(spans[1])
@@ -493,14 +514,14 @@
                 outward, part, wg_mid.at[0, :, quarter(col)], g_s.at[g], g_m.at[col], column(end),
             )
         if step == GATES - 1:
-            send_if(lacks, wg_out.at[g, :, halves], wg_via, g_s.at[g], h_r, beside)
+            send_if(lacks, wg_out.at[g, :, side(0)], wg_via, g_s.at[g], h_r, beside)
         unsent.append((plane != z, wg_out.at[g], g_s.at[g]))
 
     def nearby(step):
         g, plane = gate_of(step)
-        for col in range(nr):
+        for n, col in enumerate(away):
             go = jnp.logical_and(outer, plane == hub)
-            if step == GATES - 1 and col >= nr // 2:
+            if step == GATES - 1 and n >= nr // 2:
                 go = jnp.logical_and(go, jnp.logical_not(lacks))
             send_if(
                 go, wg_out.at[g, :, quarter(col)], wg_end.at[g, :, quarter(col)], g_s.at[g],
@@ -510,8 +531,9 @@
     def assist():
         g, _ = gate_of(GATES - 1)
         pl.when(helps)(functools.partial(landed, wg_via, h_r))
-        for col in range(nr // 2, nr):
-            part = wg_via.at[:, (col - nr // 2) * cw : (col - nr // 2 + 1) * cw]
+        for n in range(nr // 2):
+            col = 2 * ((x + 1) % nx) + n
+            part = wg_via.at[:, n * cw : (n + 1) * cw]
             where = place(2 * hub + y, 2 * ((x + 1) % nx) + c)
             send_if(helps, part, wg_end.at[g, :, quarter(col)], h_s, g_e.at[g * nr + col], where)
         unsent.append((helps, wg_via, h_s))
@@ -557,7 +579,7 @@
         g, plane = gate_of(step)
         passed = jnp.logical_and(inner, jnp.logical_and(plane != z, plane != end))
         far = (plane // half != high) & ((plane == 0) | (plane == nz - 1))
-        for col in numbers:
+        for col in (away[n] for n in numbers):
             cols = quarter(col)
 
             @pl.when(passed)
@@ -593,10 +615,10 @@
     hand_on(0, (2,))
     turn(0)
     hand_on(0, (3,))
+    gather_stats()
+    turn(1)
     for n in range(GATES):
         nearby(n)
-    gather_stats()
-    turn(1)
     assist()
     for step in range(1, GATES):
         hand_on(step, range(nr))
@@ -606,7 +628,7 @@
     _, g, found = origin(0)
     b = nh * g + k
     owner, i = b // GATES, b % GATES
-    for col in range(nr):
+    for col in away:
         cols = quarter(col)
 
         @pl.when(found)

time: 48 us -> 47.5 us (0.990); the launches traced: 47.3 us -> 47.3 us
  no operation moved by 1% of the time
where the time goes in v7:
time: 47.5 us; the launch traced here: 47.3 us
  Pallas kernels  46.7 us (98%)
  between operations  0.64 us (1%)
    pallas_call x1, Pallas kernels, by_hidden(): pl.pallas_call(functools.partial(kernel, ns, nr), out_shape=(pltpu.VMEM((...  45.8 us

profile of v7, /device:TPU:1, one launch (start us, length us, event | category | flops | bytes accessed | tf_op | source)
XLA Modules:
  0.0 47.3 jit_solution(6770342294213068058)
XLA Ops:
  0.6 45.8 %shard_map.94 = (bf16[128,1024]{1,0:T(8,128)(2,1)S(1)}, f32[384,256]{1,0:T(8,128)S(1)}, f32[6,1024]{1,0:T(8,128)S(1)}) custom-call(bf16[128,1024]{1,0:T(8,128)(2,1)} %bitcast.5, bf16[384,256]{1,0:T(8,128)(2,1)} %weight_hbm.1, f32[128,1024]{1,0:T(8,128)} %bitcast.4, s32[1,128]{1,0:T(1,128)} %ids_hbm.1, f32[3,1024]{1,0:T(4,128)} %recur_hbm.1, ...), custom_call_target="tpu_custom_call" | custom-call | tf_op jit(solution)/shard_map/pallas_call | solution.py:765
  46.5 0.9 %shard_map.95 = (bf16[128,1024]{1,0:T(8,128)(2,1)}, f32[384,256]{1,0:T(8,128)}, f32[6,1024]{1,0:T(8,128)}) custom-call(bf16[128,1024]{1,0:T(8,128)(2,1)S(1)} %get-tuple-element.9.in_a, f32[384,256]{1,0:T(8,128)S(1)} %get-tuple-element.10.in_b, f32[6,1024]{1,0:T(8,128)S(1)} %get-tuple-element.11.in_c), custom_call_target="tpu_custom_call" | custom-call | tf_op jit(solution)/shard_map/pallas_call | solution.py:780

commit v8 on v7

--- a/solution.py
+++ b/solution.py
@@ -172,13 +172,16 @@
     pl.semaphore_wait(barrier, nh - 1 + nz - 1)
 
     mine = pl.ds(pl.multiple_of(r * cw, cw), cw)
+    kept = jnp.int32(0)
     for i in range(GATES):
         b = GATES * s + i
         g, j = b // nh, b % nh
         part = weight.at[i * hb : (i + 1) * hb, :]
-        send_or_local(part, piece(g, mine), w_s.at[i], w_r.at[g * nr + r], at(z, j), j == k)
-        unsent.append((j != k, part, w_s.at[i]))
-
+        send_or_local(part, piece(g, mine), w_s, w_r.at[g * nr + r], at(z, j), j == k)
+        kept = kept + (j == k).astype(jnp.int32)
+
+    unsent.append((kept == 0, weight, w_s))
+    unsent.append((kept == 1, weight.at[0 : (GATES - 1) * hb, :], w_s))
     partner = place(s, r + 1 - 2 * c)
     nearest = place(2 * z + (y + c) % 2, 2 * ((x + 1 - c) % nx) + c)
     across = place(2 * z + (y + 1 - c) % 2, 2 * ((x + c) % nx) + c)
@@ -410,14 +413,14 @@
         seg_out[0, o : o + 1, :] = a[first, :] * a[second, :]
         seg_out[1, o : o + 1, :] = b[first, :] + a[first, :] * b[second, :]
     for plane in range(nz - 1):
-        send_if(plane < z, seg_out, seg_in.at[z], c_s, c_r.at[z], at(plane, k))
+        send_if(plane < z, seg_out, seg_in.at[z], c_s, c_r.at[(z + nz - 1) % nz], at(plane, k))
         unsent.append((z == plane + 1, seg_in.at[0 : plane + 1], c_s))
     carry[...] = jnp.zeros(carry.shape, F32)
     for plane in reversed(range(1, nz)):
 
         @pl.when(plane > z)
         def _():
-            landed(seg_in.at[plane], c_r.at[plane])
+            landed(seg_in.at[plane], c_r.at[plane - 1])
             carry[0:nr, :] = seg_in[plane, 1, 0:nr, :] + seg_in[plane, 0, 0:nr, :] * carry[0:nr, :]
 
     into = carry[0:nr, :]
@@ -507,15 +510,14 @@
                 product(spans[1])
             part = wg_out.at[g, :, quarter(col)]
             send_if(
-                jnp.logical_and(inward, plane != hub), part, wg_end.at[g, :, quarter(col)], g_s.at[g],
+                jnp.logical_and(inward, plane != hub), part, wg_end.at[g, :, quarter(col)], g_s,
                 g_e.at[g * nr + col], column(hub),
             )
             send_if(
-                outward, part, wg_mid.at[0, :, quarter(col)], g_s.at[g], g_m.at[col], column(end),
+                outward, part, wg_mid.at[0, :, quarter(col)], g_s, g_m.at[col], column(end),
             )
         if step == GATES - 1:
-            send_if(lacks, wg_out.at[g, :, side(0)], wg_via, g_s.at[g], h_r, beside)
-        unsent.append((plane != z, wg_out.at[g], g_s.at[g]))
+            send_if(lacks, wg_out.at[g, :, side(0)], wg_via, g_s, h_r, beside)
 
     def nearby(step):
         g, plane = gate_of(step)
@@ -524,7 +526,7 @@
             if step == GATES - 1 and n >= nr // 2:
                 go = jnp.logical_and(go, jnp.logical_not(lacks))
             send_if(
-                go, wg_out.at[g, :, quarter(col)], wg_end.at[g, :, quarter(col)], g_s.at[g],
+                go, wg_out.at[g, :, quarter(col)], wg_end.at[g, :, quarter(col)], g_s,
                 g_e.at[g * nr + col], column(hub),
             )
 
@@ -590,7 +592,7 @@
             for slot, there in enumerate((jnp.logical_not(far), far)):
                 send_if(
                     jnp.logical_and(passed, there), wg_out.at[g, :, cols], wg_mid.at[slot, :, cols],
-                    g_s.at[g], g_m.at[slot * nr + col], column(plane),
+                    g_s, g_m.at[slot * nr + col], column(plane),
                 )
 
     weigh(0)
@@ -625,6 +627,8 @@
     unsent.append((True, part_out, d_s))
     unsent.append((True, fin_out, f_s))
 
+    unsent.append((found0, wg_out.at[0 : GATES - 1], g_s))
+    unsent.append((jnp.logical_not(found0), wg_out, g_s))
     _, g, found = origin(0)
     b = nh * g + k
     owner, i = b // GATES, b % GATES
@@ -654,11 +658,11 @@
 
         @pl.when(jnp.logical_and(found, here))
         def _():
-            local(wg_out.at[g, :, cols], wg_in.at[i], g_r.at[i])
+            local(wg_out.at[g, :, cols], wg_in.at[i], g_r)
 
         send_if(
             jnp.logical_and(found, jnp.logical_not(here)), wg_out.at[g, :, cols], wg_in.at[i],
-            g_f, g_r.at[i], place(owner, col),
+            g_f, g_r, place(owner, col),
         )
     unsent.append((jnp.logical_and(found, owner != s), wg_out.at[0], g_f))
     unsent.append((jnp.logical_and(found, owner == s), wg_out.at[0, :, 0 : (nr - 1) * cw], g_f))
@@ -675,8 +679,8 @@
     total = total + fin_in[1].astype(F32) + fin_in[2].astype(F32)
     out_in[...] = total.astype(BF16)
 
+    landed(wg_in, g_r)
     for i in range(GATES):
-        landed(wg_in.at[i], g_r.at[i])
         block = slice(i * hb, (i + 1) * hb)
         out_w[block, :] = wg_in[i].astype(F32) * scale
 
@@ -757,8 +761,8 @@
     ]
     dma = pltpu.SemaphoreType.DMA
     counts = [
-        7, None, nh, GATES, nz - 1, GATES * nr, None, None, None, None, None, None, None, None, None, nz,
-        None, 3, None, 5, GATES, GATES * nr, 2 * nr, None, GATES, None, None, None, None, None, None,
+        7, None, nh, None, nz - 1, GATES * nr, None, None, None, None, None, None, None, None, None, nz - 1,
+        None, 3, None, 5, None, GATES * nr, 2 * nr, None, None, None, None, None, None, None, None,
     ]
     sems = [dma if n is None else dma((n,)) for n in counts]
     whole = pl.BlockSpec(memory_space=pltpu.VMEM)

time: 47.5 us -> 47.4 us (level)
  no operation moved by 1% of the time
where the time goes in v8:
time: 47.4 us; the launch traced here: 47.3 us
  Pallas kernels  46.6 us (98%)
  between operations  0.64 us (1%)
    pallas_call x1, Pallas kernels, by_hidden(): pl.pallas_call(functools.partial(kernel, ns, nr), out_shape=(pltpu.VMEM((...  45.8 us

profile of v8, /device:TPU:1, one launch (start us, length us, event | category | flops | bytes accessed | tf_op | source)
XLA Modules:
  0.0 47.3 jit_solution(8702269025377636713)
XLA Ops:
  0.6 45.8 %shard_map.94 = (bf16[128,1024]{1,0:T(8,128)(2,1)S(1)}, f32[384,256]{1,0:T(8,128)S(1)}, f32[6,1024]{1,0:T(8,128)S(1)}) custom-call(bf16[128,1024]{1,0:T(8,128)(2,1)} %bitcast.5, bf16[384,256]{1,0:T(8,128)(2,1)} %weight_hbm.1, f32[128,1024]{1,0:T(8,128)} %bitcast.4, s32[1,128]{1,0:T(1,128)} %ids_hbm.1, f32[3,1024]{1,0:T(4,128)} %recur_hbm.1, ...), custom_call_target="tpu_custom_call" | custom-call | tf_op jit(solution)/shard_map/pallas_call | solution.py:769
  46.4 0.9 %shard_map.95 = (bf16[128,1024]{1,0:T(8,128)(2,1)}, f32[384,256]{1,0:T(8,128)}, f32[6,1024]{1,0:T(8,128)}) custom-call(bf16[128,1024]{1,0:T(8,128)(2,1)S(1)} %get-tuple-element.9.in_a, f32[384,256]{1,0:T(8,128)S(1)} %get-tuple-element.10.in_b, f32[6,1024]{1,0:T(8,128)S(1)} %get-tuple-element.11.in_c), custom_call_target="tpu_custom_call" | custom-call | tf_op jit(solution)/shard_map/pallas_call | solution.py:784
